TPU v7x, 128 devices: a whole 4x4x4 slice. The times are simulated.
128 devices in a mesh: gx: 8 (over z, y_hi), gy: 8 (over x, core), lev: 2 (over y_lo).
Axes of the slice: x: 4, y: 4 (y_hi: 2, y_lo: 2; y = y_hi * 2 + y_lo), z: 4, core: 2. Of those that a mesh axis runs over, the one named last changes fastest.
Arguments:
- child_field: bfloat16 [136, 1024, 2048], P('lev', 'gx', 'gy'), may hold values from -6 to 6
- parent_old: bfloat16 [90, 1024, 2048], P('lev', 'gx', 'gy'), may hold values from -6 to 6
- level_map: int32 [136], replicated, may hold values from 0 to 89, as said below
- intersection: float32 [136], replicated, may hold values from 0.1 to 0.9
- thickness: float32 [136], replicated, may hold values from 0.5 to 5
- smooth_coef: float32 [90], P('lev'), may hold values from 0.04 to 0.24
- nest_mask: int32 [1024, 2048], P('gx', 'gy'), may hold values 0 or 1
Outputs:
- parent_new: bfloat16 [90, 1024, 2048], P('lev', 'gx', 'gy')
Inputs may be any that keep to these rules, and one draw needn't show every extreme that they name: `level_map`: starts at 0, never falls, rises by at most 1 from one child level to the next, and ends at 89, so every parent level begins some child level.
All inputs are finite; a program needn't handle non-finite values. No bound on the sum of `nest_mask` on one device may be relied on, other than what follows from the above.
Results may differ from a plain program's by a relative error of at most 0.004.
Values may be sent and summed in bfloat16 or wider, within the bound.
No kernel may reach another device: no remote copies, remote signals or barrier semaphores. Data moves between devices by JAX's collectives and lax.ppermute only.
A program may use at most 128 MiB of HBM per device.

v0:
```python
import functools

import jax
import jax.numpy as jnp
from jax import lax
from jax.experimental import pallas as pl
from jax.experimental.pallas import tpu as pltpu
from jax.sharding import PartitionSpec as P

SMOOTH = 4
LANES = 128
SUB = 8
SLOT = 24
PER_TILE = 5
PER_SENT = 3
SMALL_RUNG = 1
ROW_BLOCK = 32
F32 = jnp.float32
BF16 = jnp.bfloat16
VMEM_MIB = 1 << 20


def normed_weights(level_map, intersection, thickness, parent_total):
    parents = jnp.arange(parent_total, dtype=jnp.int32)[:, None]
    upper_level = jnp.minimum(level_map + 1, parent_total - 1)[None, :]
    raw_weight = jnp.where(parents == level_map[None, :], intersection * thickness, 0.0)
    raw_weight = raw_weight + jnp.where(
        parents == upper_level, (1.0 - intersection) * thickness, 0.0
    )
    return (raw_weight / jnp.sum(raw_weight, axis=1, keepdims=True)).astype(BF16)


def pair_swap(x, axis, parity):
    route = []
    for low in range(parity, lax.axis_size(axis) - 1, 2):
        route += [(low, low + 1), (low + 1, low)]
    return lax.ppermute(x, axis, route)


def call(kernel, grid, in_specs, out_specs, out_shape, scratch=(), flops=1, limit=24):
    return pl.pallas_call(
        kernel,
        grid=grid,
        in_specs=in_specs,
        out_specs=out_specs,
        out_shape=out_shape,
        scratch_shapes=list(scratch),
        compiler_params=pltpu.CompilerParams(vmem_limit_bytes=limit * VMEM_MIB),
        cost_estimate=pl.CostEstimate(flops=flops, bytes_accessed=1 << 20, transcendentals=0),
    )


def smem():
    return pl.BlockSpec(memory_space=pltpu.SMEM)


def whole(*shape):
    return pl.BlockSpec(shape, lambda *_: (0,) * len(shape))


def partner_kernel(count, spans, weights, child, out):
    children = child.shape[0]

    def level(j, carry):
        def add(k, total):
            return total + weights[j * children + k] * child[k].astype(F32)

        zero = jnp.zeros(child.shape[1:], F32)
        out[j] = lax.fori_loop(spans[2 * j], spans[2 * j + 1], add, zero).astype(BF16)
        return carry

    lax.fori_loop(0, count, level, 0)


def scan_children(info, slots, shares, loads, stores, zero_store, parents):
    children = slots.shape[0] - 1
    zeros = [jnp.zeros_like(x) for x in loads(0)]

    def clear(p, carry):
        zero_store(p)
        return carry

    lax.fori_loop(0, info[5], clear, 0)
    lax.fori_loop(info[6], parents, clear, 0)

    def step(k, state):
        here, above = state
        rose = shares[2 * children + k]
        kept = 1.0 - rose
        low, high = shares[k], shares[children + k]
        values = loads(k)
        here = [kept * h + rose * a + low * v for h, a, v in zip(here, above, values)]
        above = [kept * a + high * v for a, v in zip(above, values)]
        stores(slots[k], here)
        return here, above

    here, above = lax.fori_loop(0, children, step, (zeros, zeros), unroll=4)
    stores(slots[children], above)


def rows_kernel(
    parents, count, info, slots, shares,
    child_t, child_b, par_t, par_b, mask_t, mask_b, part_t, part_b, even, odd, top, bot,
):
    def loads(k):
        return [child_t[k].astype(F32), child_b[k].astype(F32)]

    def stores(slot, values):
        top[slot], bot[slot] = values

    def zero_store(p):
        top[p] = jnp.zeros(top.shape[1:], F32)
        bot[p] = jnp.zeros(bot.shape[1:], F32)

    scan_children(info, slots, shares, loads, stores, zero_store, parents)

    def add_partner(j, carry):
        p = info[2] + j
        top[p] += part_t[j].astype(F32)
        bot[p] += part_b[j].astype(F32)
        return carry

    lax.fori_loop(0, count, add_partner, 0)
    row = lax.broadcasted_iota(jnp.int32, top.shape[1:], 0)
    flip = info[0] == 1
    fed_t, fed_b = mask_t[...] != 0, mask_b[...] != 0

    def pair(m, carry):
        p, q = 2 * m, jnp.minimum(2 * m + 1, parents - 1)
        tops = [jnp.where(fed_t, top[i], par_t[i].astype(F32)) for i in (p, q)]
        bots = [jnp.where(fed_b, bot[i], par_b[i].astype(F32)) for i in (p, q)]
        first = jnp.where(row < SMOOTH, tops[0], pltpu.roll(tops[1], SMOOTH, 0))
        last = jnp.where(row < SMOOTH, pltpu.roll(bots[0], SMOOTH, 0), bots[1])
        even[m] = jnp.where(flip, first, last).astype(BF16)
        odd[m] = jnp.where(flip, last, first).astype(BF16)
        return carry

    lax.fori_loop(0, even.shape[0], pair, 0, unroll=2)


def field_kernel(
    parents, count, info, slots, shares, child, par, mask, part, field, edge, sent, acc
):
    def loads(k):
        return [child[k].astype(F32)]

    def stores(slot, values):
        acc[slot] = values[0]

    def zero_store(p):
        acc[p] = jnp.zeros(acc.shape[1:], F32)

    scan_children(info, slots, shares, loads, stores, zero_store, parents)

    def add_partner(j, carry):
        acc[info[2] + j] += part[j].astype(F32)
        return carry

    lax.fori_loop(0, count, add_partner, 0)
    fed = mask[...] != 0

    def blend(p, carry):
        field[p] = jnp.where(fed, acc[p], par[p].astype(F32)).astype(BF16)
        return carry

    lax.fori_loop(0, parents, blend, 0, unroll=3)
    edges = make_edges(parents, lambda p: field[p].astype(F32))
    for t, tile in enumerate(edges):
        edge[t] = tile.astype(BF16)
    for t, tile in enumerate(make_sent(edges)):
        sent[t] = tile.astype(BF16)


def make_edges(parents, load):
    tiles = []
    for t in range(pl.cdiv(parents, PER_TILE)):
        tile = None
        for j in range(min(PER_TILE, parents - t * PER_TILE)):
            value = load(t * PER_TILE + j)
            lane = lax.broadcasted_iota(jnp.int32, (value.shape[0], LANES), 1) - SLOT * j
            last = pltpu.roll(value[:, -LANES:], (SLOT * j + 8) % LANES, 1)
            first = pltpu.roll(value[:, :LANES], (SLOT * j + 16) % LANES, 1)
            both = jnp.where(lane < 12, last, first)
            tile = both if tile is None else jnp.where(lane >= 0, both, tile)
        tiles.append(tile)
    return tiles


def make_sent(edges):
    tiles = []
    for q in range(pl.cdiv(len(edges), PER_SENT)):
        tile = None
        for u, edge in enumerate(edges[q * PER_SENT : (q + 1) * PER_SENT]):
            lane = lax.broadcasted_iota(jnp.int32, edge.shape, 1) % SLOT - 8 * u
            last = pltpu.roll(edge, (8 * u - 4) % LANES, 1)
            first = pltpu.roll(edge, (8 * u - 12) % LANES, 1)
            both = jnp.where(lane < 4, last, first)
            tile = both if tile is None else jnp.where(lane >= 0, both, tile)
        tiles.append(tile)
    return tiles


def halo_kernel(parents, info, even, odd, sent_core, halo, edge, sent):
    flip = info[0] == 1
    row = lax.broadcasted_iota(jnp.int32, halo.shape[1:], 0)

    def load(p):
        a, b = even[p // 2].astype(F32), odd[p // 2].astype(F32)
        after, before = jnp.where(flip, b, a), jnp.where(flip, a, b)
        if p % 2 == 0:
            before = pltpu.roll(before, SMOOTH, 0)
        else:
            after = pltpu.roll(after, SMOOTH, 0)
        value = jnp.where(row < SMOOTH, after, before)
        halo[p] = value.astype(BF16)
        return value

    edges = make_edges(parents, load)
    for t, tile in enumerate(edges):
        edge[t] = tile.astype(BF16)
    rows = sent_core.shape[1]
    sent[:, :rows, :] = sent_core[...]
    for t, tile in enumerate(make_sent(edges)):
        sent[t, rows:, :] = tile.astype(BF16)


def row_sweep(values, side_sum, scales, keeps):
    count = len(values)
    before = pltpu.roll(values[-1], 1, 0)
    after = pltpu.roll(values[0], SUB - 1, 0)
    out = []
    for i, value in enumerate(values):
        up = values[i - 1] if i > 0 else before
        down = values[i + 1] if i < count - 1 else after
        out.append(keeps[i] * value + scales[i] * ((up + down) + side_sum(i, value)))
    return out


def row_flags(info, count, rows):
    sub = lax.broadcasted_iota(jnp.int32, (SUB, LANES), 0)
    flags = []
    for i in range(count):
        r = (SUB - 1) * count + i - rows
        if r < 0:
            flags.append(None)
            continue
        inside = info[4] if r < SMOOTH else info[3]
        flags.append(jnp.where(sub == SUB - 1, inside.astype(F32), 1.0))
    return flags


def smooth_kernel(info, coefs, field, halo, out, left, right):
    levels, rows = field.shape[:2]
    count = left.shape[0] // SUB
    lane = lax.broadcasted_iota(jnp.int32, (SUB, LANES), 1)
    flags = row_flags(info, count, rows)
    base = pl.program_id(0) * levels

    def level(p, carry):
        scale = coefs[base + p]
        keep = 1.0 - 4.0 * scale
        scales = [scale if f is None else scale * f for f in flags]
        keeps = [keep if f is None else keep * f for f in flags]
        for ref, cut in ((left, slice(0, LANES)), (right, slice(LANES, 2 * LANES))):
            ref[:rows, :] = field[p, :, cut].astype(F32)
            ref[rows:, :] = halo[p, :, cut].astype(F32)
        a = [left[pl.ds(i, SUB, stride=count), :] for i in range(count)]
        b = [right[pl.ds(i, SUB, stride=count), :] for i in range(count)]
        for _ in range(SMOOTH):
            ups = [(pltpu.roll(x, 1, 1), pltpu.roll(y, 1, 1)) for x, y in zip(a, b)]
            dns = [
                (pltpu.roll(x, LANES - 1, 1), pltpu.roll(y, LANES - 1, 1)) for x, y in zip(a, b)
            ]
            sides = [
                (ua + jnp.where(lane == LANES - 1, db, da), jnp.where(lane == 0, ua, ub) + db)
                for (ua, ub), (da, db) in zip(ups, dns)
            ]
            a = row_sweep(a, lambda i, _: sides[i][0], scales, keeps)
            b = row_sweep(b, lambda i, _: sides[i][1], scales, keeps)
        for i in range(count):
            left[pl.ds(i, SUB, stride=count), :] = a[i]
            right[pl.ds(i, SUB, stride=count), :] = b[i]
        out[p, :, :LANES] = left[:rows, :].astype(BF16)
        out[p, :, LANES:] = right[:rows, :].astype(BF16)
        return carry

    lax.fori_loop(0, levels, level, 0)


def seam_kernel(info, coefs, even, odd, core, edge, main, out, tiles, work):
    total = tiles.shape[0]
    rows = core.shape[1]
    count = tiles.shape[1] // SUB
    step = pl.program_id(0)

    @pl.when(step == 0)
    def _():
        flip = info[1] == 1
        flags = row_flags(info, count, rows)
        slot = lax.broadcasted_iota(jnp.int32, tiles.shape[1:], 1) % SLOT
        for q in range(even.shape[0]):
            a, b = even[q].astype(F32), odd[q].astype(F32)
            after, before = jnp.where(flip, b, a), jnp.where(flip, a, b)
            for u in range(min(PER_SENT, total - q * PER_SENT)):
                t = q * PER_SENT + u
                own = jnp.concatenate([core[t].astype(F32), edge[t].astype(F32)], axis=0)
                right = pltpu.roll(after, (4 - 8 * u) % LANES, 1)
                left = pltpu.roll(before, (12 - 8 * u) % LANES, 1)
                tile = jnp.where(slot < 12, right, left)
                tiles[t] = jnp.where((slot >= 8) & (slot < 16), tile, own)
        for t in range(total):
            for i in range(count):
                work[0, t, i] = tiles[t, pl.ds(i, SUB, stride=count), :]
        for s in range(SMOOTH):
            for t in range(total):
                scale = coefs[0, t]
                keep = coefs[1, t]
                scales = [scale if f is None else scale * f for f in flags]
                keeps = [keep if f is None else keep * f for f in flags]
                values = [work[s % 2, t, i] for i in range(count)]
                new = row_sweep(
                    values,
                    lambda _, x: pltpu.roll(x, 1, 1) + pltpu.roll(x, LANES - 1, 1),
                    scales,
                    keeps,
                )
                for i in range(count):
                    if s < SMOOTH - 1:
                        work[(s + 1) % 2, t, i] = new[i]
                    else:
                        tiles[t, pl.ds(i, SUB, stride=count), :] = new[i]

    seam = tiles[step, :rows, :]
    lane = lax.broadcasted_iota(jnp.int32, seam.shape, 1)
    for j in range(main.shape[0]):
        first = pltpu.roll(seam, (-SLOT * j - 16) % LANES, 1)
        last = pltpu.roll(seam, (120 - SLOT * j) % LANES, 1)
        a, b = main[j, :, :LANES].astype(F32), main[j, :, LANES:].astype(F32)
        out[j, :, :LANES] = jnp.where(lane < SMOOTH, first, a).astype(BF16)
        out[j, :, LANES:] = jnp.where(lane >= LANES - SMOOTH, last, b).astype(BF16)


def feed_back(count, child, parent, normed, level_map, smooth_coef, mask):
    children, rows, columns = child.shape
    parents = parent.shape[0]
    total = normed.shape[0]
    slab = lax.axis_index("lev")
    gx, gy = lax.axis_index("gx"), lax.axis_index("gy")
    own_map = lax.dynamic_slice_in_dim(level_map, slab * children, children)
    own = lax.dynamic_slice_in_dim(normed, slab * children, children, 1).astype(F32)
    levels = jnp.arange(total, dtype=jnp.int32)[:, None]
    low = jnp.sum(jnp.where(levels == own_map, own, 0.0), axis=0)
    high = jnp.sum(jnp.where(levels == own_map + 1, own, 0.0), axis=0)
    rose = jnp.concatenate([jnp.zeros((1,), F32), (own_map[1:] != own_map[:-1]).astype(F32)])
    shares = jnp.concatenate([low, high, rose])
    place = jnp.concatenate([own_map, own_map[-1:] + 1]) - slab * parents
    slots = jnp.where((place >= 0) & (place < parents), place, parents)
    start = jnp.where(slab == 0, parents, parents - count)
    window = start + jnp.arange(count, dtype=jnp.int32)[:, None]
    spans = jnp.concatenate(
        [
            jnp.sum((own_map < window - 1).astype(jnp.int32), axis=1, keepdims=True),
            jnp.sum((own_map <= window).astype(jnp.int32), axis=1, keepdims=True),
        ],
        axis=1,
    ).reshape(-1)
    weights = lax.dynamic_slice_in_dim(own, start, count, 0).reshape(-1)
    info = jnp.stack(
        [
            gx % 2,
            gy % 2,
            jnp.where(slab == 0, parents - count, 0),
            (gx > 0).astype(jnp.int32),
            (gx < lax.axis_size("gx") - 1).astype(jnp.int32),
            jnp.clip(place[0], 0, parents),
            jnp.clip(place[-1] + 1, 0, parents),
        ]
    ).astype(jnp.int32)

    block = ROW_BLOCK
    part = call(
        functools.partial(partner_kernel, count),
        (rows // block,),
        [smem(), smem(), pl.BlockSpec((children, block, columns), lambda i: (0, i, 0))],
        pl.BlockSpec((count, block, columns), lambda i: (0, i, 0)),
        jax.ShapeDtypeStruct((count, rows, columns), BF16),
    )(spans, weights, child)
    part = pair_swap(part, "lev", 0)

    ends = rows // SUB - 1

    def two(lead):
        return [
            pl.BlockSpec((lead, SUB, columns), lambda i: (0, 0, 0)),
            pl.BlockSpec((lead, SUB, columns), lambda i: (0, ends, 0)),
        ]

    packed = pl.cdiv(parents, 2)
    strip = jax.ShapeDtypeStruct((packed, SUB, columns), BF16)
    row_even, row_odd = call(
        functools.partial(rows_kernel, parents, count),
        (1,),
        [
            smem(), smem(), smem(),
            *two(children),
            *two(parents),
            pl.BlockSpec((SUB, columns), lambda i: (0, 0)),
            pl.BlockSpec((SUB, columns), lambda i: (ends, 0)),
            *two(count),
        ],
        [whole(packed, SUB, columns)] * 2,
        [strip, strip],
        [pltpu.VMEM((parents + 1, SUB, columns), F32)] * 2,
    )(info, slots, shares, child, child, parent, parent, mask, mask, part, part)
    row_even = pair_swap(row_even, "gx", 0)
    row_odd = pair_swap(row_odd, "gx", 1)

    seams = pl.cdiv(parents, PER_TILE)
    sents = pl.cdiv(seams, PER_SENT)
    field, edge_core, sent_core = call(
        functools.partial(field_kernel, parents, count),
        (rows // block,),
        [
            smem(), smem(), smem(),
            pl.BlockSpec((children, block, columns), lambda i: (0, i, 0)),
            pl.BlockSpec((parents, block, columns), lambda i: (0, i, 0)),
            pl.BlockSpec((block, columns), lambda i: (i, 0)),
            pl.BlockSpec((count, block, columns), lambda i: (0, i, 0)),
        ],
        [
            pl.BlockSpec((parents, block, columns), lambda i: (0, i, 0)),
            pl.BlockSpec((seams, block, LANES), lambda i: (0, i, 0)),
            pl.BlockSpec((sents, block, LANES), lambda i: (0, i, 0)),
        ],
        [
            jax.ShapeDtypeStruct((parents, rows, columns), BF16),
            jax.ShapeDtypeStruct((seams, rows, LANES), BF16),
            jax.ShapeDtypeStruct((sents, rows, LANES), BF16),
        ],
        [pltpu.VMEM((parents + 1, block, columns), F32)],
        flops=1 << 34,
    )(info, slots, shares, child, parent, mask, part)

    extended = rows + SUB
    halo, edge_halo, sent = call(
        functools.partial(halo_kernel, parents),
        (1,),
        [smem(), whole(packed, SUB, columns), whole(packed, SUB, columns), whole(sents, rows, LANES)],
        [whole(parents, SUB, columns), whole(seams, SUB, LANES), whole(sents, extended, LANES)],
        [
            jax.ShapeDtypeStruct((parents, SUB, columns), BF16),
            jax.ShapeDtypeStruct((seams, SUB, LANES), BF16),
            jax.ShapeDtypeStruct((sents, extended, LANES), BF16),
        ],
    )(info, row_even, row_odd, sent_core)
    column_even = pair_swap(sent, "gy", 0)
    column_odd = pair_swap(sent, "gy", 1)

    group = PER_TILE
    main = call(
        smooth_kernel,
        (parents // group,),
        [
            smem(), smem(),
            pl.BlockSpec((group, rows, columns), lambda i: (i, 0, 0)),
            pl.BlockSpec((group, SUB, columns), lambda i: (i, 0, 0)),
        ],
        pl.BlockSpec((group, rows, columns), lambda i: (i, 0, 0)),
        jax.ShapeDtypeStruct((parents, rows, columns), BF16),
        [pltpu.VMEM((extended, LANES), F32)] * 2,
        flops=1 << 34,
    )(info, smooth_coef, field, halo)

    lane = jnp.arange(LANES, dtype=jnp.int32)
    place_in_slot = lane % SLOT
    inside = lane < SLOT * PER_TILE
    after = (place_in_slot >= 8) & (place_in_slot < 12)
    before = (place_in_slot >= 12) & (place_in_slot < 16)
    inside &= ~after | (gy < lax.axis_size("gy") - 1)
    inside &= ~before | (gy > 0)
    by_tile = jnp.repeat(smooth_coef.reshape(seams, PER_TILE), SLOT, axis=1)
    by_tile = jnp.pad(by_tile, ((0, 0), (0, LANES - SLOT * PER_TILE)))
    lane_coefs = jnp.where(inside, jnp.stack([by_tile, 1.0 - 4.0 * by_tile]), 0.0)
    lane_coefs = jnp.broadcast_to(lane_coefs[:, :, None, :], (2, seams, SUB, LANES))
    return call(
        seam_kernel,
        (seams,),
        [
            smem(),
            whole(2, seams, SUB, LANES),
            whole(sents, extended, LANES),
            whole(sents, extended, LANES),
            whole(seams, rows, LANES),
            whole(seams, SUB, LANES),
            pl.BlockSpec((group, rows, columns), lambda i: (i, 0, 0)),
        ],
        pl.BlockSpec((group, rows, columns), lambda i: (i, 0, 0)),
        jax.ShapeDtypeStruct((parents, rows, columns), BF16),
        [
            pltpu.VMEM((seams, extended, LANES), F32),
            pltpu.VMEM((2, seams, extended // SUB, SUB, LANES), F32),
        ],
    )(info, lane_coefs, column_even, column_odd, edge_core, edge_halo, main)


def shards(child_field, parent_old, level_map, intersection, thickness, smooth_coef, nest_mask):
    children, parents = child_field.shape[0], parent_old.shape[0]
    total = parents * lax.axis_size("lev")
    normed = normed_weights(level_map, intersection, thickness, total)
    most = children - parents + 1
    crossing = jnp.maximum(level_map[children - 1] + 2 - parents, parents - level_map[children])

    def run(count):
        return lambda: feed_back(
            count, child_field, parent_old, normed, level_map, smooth_coef, nest_mask
        )

    return lax.cond(crossing <= SMALL_RUNG, run(SMALL_RUNG), run(most))


def solution(mesh):
    in_specs = (P("lev", "gx", "gy"), P("lev", "gx", "gy"), P(), P(), P(), P("lev"), P("gx", "gy"))
    out_specs = P("lev", "gx", "gy")
    return jax.shard_map(shards, mesh=mesh, in_specs=in_specs, out_specs=out_specs, check_vma=False)
```

profile of v0, /device:TPU:49, one launch (start us, length us, event | category | flops | bytes accessed | tf_op | source)
XLA Modules:
  0.0 67.0 jit_solution(17303427611681144262)
XLA Ops:
  0.0 0.7 %fusion.5 = (f32[136]{0:T(256)S(1)}, f32[136]{0:T(256)S(1)}) fusion(f32[136]{0:T(256)} %param.12, f32[136]{0:T(256)} %param.13), kind=kLoop, calls=%fused_computation.51 | loop fusion | flops 408 | bytes 2176 | tf_op jit(solution)/shard_map/mul | solution.py:26
  0.7 0.7 %add_minimum_fusion = s32[136]{0:T(256)S(1)} fusion(s32[136]{0:T(256)} %param.11), kind=kLoop, calls=%fused_computation.48 | loop fusion | flops 272 | bytes 1088 | tf_op jit(solution)/shard_map/min | solution.py:25
  1.4 0.8 %fusion.2 = f32[90]{0:T(128)S(1)} fusion(f32[136]{0:T(256)S(1)} %get-tuple-element.103, s32[136]{0:T(256)S(1)} %add_minimum_fusion, f32[136]{0:T(256)S(1)} %get-tuple-element.102, s32[136]{0:T(256)} %param.11), kind=kLoop, calls=%fused_computation.45 | loop fusion | flops 73350 | bytes 2536 | tf_op jit(solution)/shard_map/reduce_sum | solution.py:30
  2.2 0.8 %divide_convert_fusion = bf16[90,136]{1,0:T(8,128)(2,1)S(1)} fusion(f32[90]{0:T(128)S(1)} %fusion.2, f32[136]{0:T(256)S(1)} %get-tuple-element.103, s32[136]{0:T(256)S(1)} %add_minimum_fusion, f32[136]{0:T(256)S(1)} %get-tuple-element.102, s32[136]{0:T(256)} %param.11), kind=kLoop, calls=%fused_computation.42 | loop fusion | flops 85680 | bytes 27016 | tf_op jit(solution)/shard_map/convert_element_type | solution.py:30
  3.0 1.4 %fusion.6 = (s32[1]{0:T(128)}, s32[1]{0:T(128)}) fusion(s32[136]{0:T(256)} %param.11), kind=kLoop, calls=%fused_computation.52 | loop fusion | bytes 16 | tf_op jit(solution)/shard_map/slice | solution.py:511
  5.7 61.3 %conditional.1 = (bf16[45,128,256]{2,1,0:T(8,128)(2,1)}) conditional(s32[]{:T(128)} %bitcast.20, (s32[136]{0:T(256)}, f32[45]{0:T(128)}, bf16[90,136]{1,0:T(8,128)(2,1)S(1)}, bf16[68,128,256]{2,1,0:T(8,128)(2,1)}, bf16[45,128,256]{2,1,0:T(8,128)(2,1)}, /*index=5*/s32[128,256]{1,0:T(8,128)}) %tuple.11, (s32[136]{0:T(256)}, f32[45]{0:T(128)}, ...), branch_computations={%region_1.6_spmd, %region_6.11_spmd} | conditional | flops 34359808000 | bytes 26705468 | solution.py:518
  5.7 0.0 copy-start.5
  5.7 0.0 copy-start.1
  5.7 0.0 copy-start.3
  5.7 0.1 dynamic-slice_convert_fusion.1
  5.8 1.6 %fusion = (s32[]{:T(128)}, s32[]{:T(128)}, s32[68]{0:T(128)S(1)}) fusion(s32[]{:T(128)S(6)} %sub.32, s32[]{:T(128)S(6)} %select_n.95, s32[136]{0:T(256)} %get-tuple-element.46, s32[]{:T(128)S(6)} %select_n.88), kind=kLoop, calls=%fused_computation.36 | loop fusion | flops 406 | bytes 564 | tf_op jit(solution)/shard_map/cond/branch_1_fun/reduce_sum | solution.py:362
  7.4 1.4 %add_bitcast_fusion.spans = s32[2]{0:T(128)S(1)} fusion(s32[1,1]{1,0:T(1,128)} %bitcast.17, s32[1,1]{1,0:T(1,128)} %bitcast.16), kind=kLoop, calls=%fused_computation.39 | loop fusion | flops 2 | bytes 16 | tf_op jit(solution)/shard_map/cond/branch_1_fun/reshape | solution.py:366
  8.7 3.3 %branch_1_fun.6 = bf16[1,128,256]{2,1,0:T(8,128)(2,1)S(1)} custom-call(s32[2]{0:T(128)S(1)} %add_bitcast_fusion.spans, f32[68]{0:T(128)S(1)} %dynamic-slice_bitcast_fusion.weights, bf16[68,128,256]{2,1,0:T(8,128)(2,1)} %get-tuple-element.72.child.child_t.child_b), custom_call_target="tpu_custom_call" | custom-call | flops 1 | bytes 1048576 | tf_op jit(solution)/shard_map/cond/branch_1_fun/pallas_call | solution.py:381
  12.1 1.0 %collective-permute-start.5 = (bf16[1,128,256]{2,1,0:T(8,128)(2,1)S(1)}, bf16[1,128,256]{2,1,0:T(8,128)(2,1)S(1)}, u32[]{:S(2)}, u32[]{:S(2)}) collective-permute-start(bf16[1,128,256]{2,1,0:T(8,128)(2,1)S(1)} %branch_1_fun.6), channel_id=1, source_target_pairs={{0,1},{1,0},{2,3},{3,2},{4,5},{5,4},{6,7},{7,6},{8,9},{9,8},{10,11... | collective-permute-start | bytes 196616 | tf_op jit(solution)/shard_map/cond/branch_1_fun/ppermute | solution.py:37
  13.1 0.1 compare_convert_fusion.3
  13.1 0.6 slice.29
  13.7 0.1 select_reduce_fusion.3
  14.5 0.1 and_select_fusion.2
  14.6 0.6 fusion.4
  16.4 0.0 copy-done.5
  16.4 0.1 reshape.118
  16.4 0.1 broadcast_in_dim.74
  16.5 0.1 reshape.119
  16.7 0.1 stack.66.info
  16.8 0.1 pad_maximum_fusion.1.shares
  16.8 0.0 collective-permute-done.5.part_t.part_b.part
  16.8 0.0 copy-done.1
  16.8 0.0 copy-done.3
  16.8 1.7 %branch_1_fun.7 = (bf16[23,8,256]{2,1,0:T(8,128)(2,1)S(1)}, bf16[23,8,256]{2,1,0:T(8,128)(2,1)S(1)}) custom-call(s32[7]{0:T(128)S(1)} %stack.66.info, s32[69]{0:T(128)S(1)} %get-tuple-element.90.slots, f32[204]{0:T(256)S(1)} %pad_maximum_fusion.1.shares, bf16[68,128,256]{2,1,0:T(8,128)(2,1)} %get-tuple-element.72.child.child_t.child_b, ...), custom_call_target="tpu_custom_call" | custom-call | flops 1 | bytes 1048576 | tf_op jit(solution)/shard_map/cond/branch_1_fun/pallas_call | solution.py:400
  18.6 0.4 collective-permute-start.6
  19.0 5.9 %collective-permute-start.7 = (bf16[23,8,256]{2,1,0:T(8,128)(2,1)S(1)}, bf16[23,8,256]{2,1,0:T(8,128)(2,1)S(1)}, u32[]{:S(2)}, u32[]{:S(2)}) collective-permute-start(bf16[23,8,256]{2,1,0:T(8,128)(2,1)S(1)} %get-tuple-element.53), channel_id=1, source_target_pairs={{16,32},{32,16},{48,64},{64,48},{80,96},{96,80},{17,33},{33,17},{4... | collective-permute-start | bytes 282632 | tf_op jit(solution)/shard_map/cond/branch_1_fun/ppermute | solution.py:37
  24.9 7.3 %branch_1_fun.8 = (bf16[45,128,256]{2,1,0:T(8,128)(2,1)S(1)}, bf16[9,128,128]{2,1,0:T(8,128)(2,1)S(1)}, bf16[3,128,128]{2,1,0:T(8,128)(2,1)S(1)}) custom-call(s32[7]{0:T(128)S(1)} %stack.66.info, s32[69]{0:T(128)S(1)} %get-tuple-element.90.slots, f32[204]{0:T(256)S(1)} %pad_maximum_fusion.1.shares, ...), custom_call_target="tpu_custom_call" | custom-call | flops 17179869184 | bytes 1048576 | tf_op jit(solution)/shard_map/cond/branch_1_fun/pallas_call | solution.py:420
  32.2 0.0 collective-permute-done.6.even
  32.2 0.0 collective-permute-done.7.odd
  32.2 0.8 %branch_1_fun.9 = (bf16[45,8,256]{2,1,0:T(8,128)(2,1)S(1)}, bf16[9,8,128]{2,1,0:T(8,128)(2,1)S(1)}, bf16[3,136,128]{2,1,0:T(8,128)(2,1)S(1)}) custom-call(s32[7]{0:T(128)S(1)} %stack.66.info, bf16[23,8,256]{2,1,0:T(8,128)(2,1)S(1)} %collective-permute-done.6.even, bf16[23,8,256]{2,1,0:T(8,128)(2,1)S(1)} %collective-permute-done.7.odd, ...), custom_call_target="tpu_custom_call" | custom-call | flops 1 | bytes 1048576 | tf_op jit(solution)/shard_map/cond/branch_1_fun/pallas_call | solution.py:445
  33.0 1.6 %collective-permute-start.8 = (bf16[3,136,128]{2,1,0:T(8,128)(2,1)S(1)}, bf16[3,136,128]{2,1,0:T(8,128)(2,1)S(1)}, u32[]{:S(2)}, u32[]{:S(2)}) collective-permute-start(bf16[3,136,128]{2,1,0:T(8,128)(2,1)S(1)} %get-tuple-element.55), channel_id=1, source_target_pairs={{0,2},{2,0},{4,6},{6,4},{8,10},{10,8},{12,14},{14,12},{1,3},{3,1},... | collective-permute-start | bytes 313352 | tf_op jit(solution)/shard_map/cond/branch_1_fun/ppermute | solution.py:37
  34.5 3.0 %collective-permute-start.9 = (bf16[3,136,128]{2,1,0:T(8,128)(2,1)S(1)}, bf16[3,136,128]{2,1,0:T(8,128)(2,1)S(1)}, u32[]{:S(2)}, u32[]{:S(2)}) collective-permute-start(bf16[3,136,128]{2,1,0:T(8,128)(2,1)S(1)} %get-tuple-element.55), channel_id=1, source_target_pairs={{2,4},{4,2},{6,8},{8,6},{10,12},{12,10},{3,5},{5,3},{7,9},{9,7},{1... | collective-permute-start | bytes 313352 | tf_op jit(solution)/shard_map/cond/branch_1_fun/ppermute | solution.py:37
  37.6 23.0 %branch_1_fun.10.main = bf16[45,128,256]{2,1,0:T(8,128)(2,1)S(1)} custom-call(s32[7]{0:T(128)S(1)} %stack.66.info, f32[45]{0:T(128)S(1)} %copy-done.5, bf16[45,128,256]{2,1,0:T(8,128)(2,1)S(1)} %get-tuple-element.58.field, bf16[45,8,256]{2,1,0:T(8,128)(2,1)S(1)} %get-tuple-element.59.halo), custom_call_target="tpu_custom_call" | custom-call | flops 17179869184 | bytes 1048576 | tf_op jit(solution)/shard_map/cond/branch_1_fun/pallas_call | solution.py:460
  60.5 0.0 collective-permute-done.8.even
  60.5 0.0 collective-permute-done.9.odd
  60.6 6.4 %branch_1_fun.11 = bf16[45,128,256]{2,1,0:T(8,128)(2,1)} custom-call(s32[7]{0:T(128)S(1)} %stack.66.info, f32[2,9,8,128]{3,2,1,0:T(8,128)S(1)} %broadcast_in_dim.76.coefs, bf16[3,136,128]{2,1,0:T(8,128)(2,1)S(1)} %collective-permute-done.8.even, bf16[3,136,128]{2,1,0:T(8,128)(2,1)S(1)} %collective-permute-done.9.odd, ...), custom_call_target="tpu_custom_call" | custom-call | flops 1 | bytes 1048576 | tf_op jit(solution)/shard_map/cond/branch_1_fun/pallas_call | solution.py:485
  (6 shorter events, 0.1 us)
Async XLA Ops:
  5.7 10.7 %copy-start.5 = (f32[45]{0:T(128)S(1)}, f32[45]{0:T(128)}, u32[]{:S(2)}) copy-start(f32[45]{0:T(128)} %get-tuple-element.70.coefs) | copy-start | bytes 544 | tf_op jit(solution)/shard_map/cond
  5.7 11.2 %copy-start.1 = (bf16[45,128,256]{2,1,0:T(8,128)(2,1)S(1)}, bf16[45,128,256]{2,1,0:T(8,128)(2,1)}, u32[]{:S(2)}) copy-start(bf16[45,128,256]{2,1,0:T(8,128)(2,1)} %get-tuple-element.74.par_t.par_b.par) | copy-start | bytes 8847364 | tf_op jit(solution)/shard_map/cond
  5.7 11.1 %copy-start.3 = (s32[128,256]{1,0:T(8,128)S(1)}, s32[128,256]{1,0:T(8,128)}, u32[]{:S(2)}) copy-start(s32[128,256]{1,0:T(8,128)} %get-tuple-element.76.mask_t.mask_b.mask) | copy-start | bytes 393220 | tf_op jit(solution)/shard_map/cond
  12.1 4.8 %collective-permute-start.5 = (bf16[1,128,256]{2,1,0:T(8,128)(2,1)S(1)}, bf16[1,128,256]{2,1,0:T(8,128)(2,1)S(1)}, u32[]{:S(2)}, u32[]{:S(2)}) collective-permute-start(bf16[1,128,256]{2,1,0:T(8,128)(2,1)S(1)} %branch_1_fun.6), channel_id=1, source_target_pairs={{0,1},{1,0},{2,3},{3,2},{4,5},{5,4},{6,7},{7,6},{8,9},{9,8},{10,11... | collective-permute-start | bytes 196616 | tf_op jit(solution)/shard_map/cond/branch_1_fun/ppermute | solution.py:37
  18.6 13.6 %collective-permute-start.6 = (bf16[23,8,256]{2,1,0:T(8,128)(2,1)S(1)}, bf16[23,8,256]{2,1,0:T(8,128)(2,1)S(1)}, u32[]{:S(2)}, u32[]{:S(2)}) collective-permute-start(bf16[23,8,256]{2,1,0:T(8,128)(2,1)S(1)} %get-tuple-element.52), channel_id=1, source_target_pairs={{0,16},{16,0},{32,48},{48,32},{64,80},{80,64},{96,112},{112,96},{1... | collective-permute-start | bytes 282632 | tf_op jit(solution)/shard_map/cond/branch_1_fun/ppermute | solution.py:37
  19.0 13.2 %collective-permute-start.7 = (bf16[23,8,256]{2,1,0:T(8,128)(2,1)S(1)}, bf16[23,8,256]{2,1,0:T(8,128)(2,1)S(1)}, u32[]{:S(2)}, u32[]{:S(2)}) collective-permute-start(bf16[23,8,256]{2,1,0:T(8,128)(2,1)S(1)} %get-tuple-element.53), channel_id=1, source_target_pairs={{16,32},{32,16},{48,64},{64,48},{80,96},{96,80},{17,33},{33,17},{4... | collective-permute-start | bytes 282632 | tf_op jit(solution)/shard_map/cond/branch_1_fun/ppermute | solution.py:37
  33.0 27.6 %collective-permute-start.8 = (bf16[3,136,128]{2,1,0:T(8,128)(2,1)S(1)}, bf16[3,136,128]{2,1,0:T(8,128)(2,1)S(1)}, u32[]{:S(2)}, u32[]{:S(2)}) collective-permute-start(bf16[3,136,128]{2,1,0:T(8,128)(2,1)S(1)} %get-tuple-element.55), channel_id=1, source_target_pairs={{0,2},{2,0},{4,6},{6,4},{8,10},{10,8},{12,14},{14,12},{1,3},{3,1},... | collective-permute-start | bytes 313352 | tf_op jit(solution)/shard_map/cond/branch_1_fun/ppermute | solution.py:37
  34.5 26.0 %collective-permute-start.9 = (bf16[3,136,128]{2,1,0:T(8,128)(2,1)S(1)}, bf16[3,136,128]{2,1,0:T(8,128)(2,1)S(1)}, u32[]{:S(2)}, u32[]{:S(2)}) collective-permute-start(bf16[3,136,128]{2,1,0:T(8,128)(2,1)S(1)} %get-tuple-element.55), channel_id=1, source_target_pairs={{2,4},{4,2},{6,8},{8,6},{10,12},{12,10},{3,5},{5,3},{7,9},{9,7},{1... | collective-permute-start | bytes 313352 | tf_op jit(solution)/shard_map/cond/branch_1_fun/ppermute | solution.py:37
where the time goes:
time: 67.4 us; the launch traced here: 67 us
  Pallas kernels  42.4 us (63%)
  starting transfers between devices  11.9 us (18%)
  other arithmetic  6.36 us (9%)
  local copies, waits for them, and re-layouts  2.92 us (4%)
  loops' own time  2.07 us (3%)
  between operations  1.29 us (2%)
    pallas_call x1, Pallas kernels, feed_back(): call(smooth_kernel, (parents // group,), [smem(), smem(), pl.BlockSpec((g...  23 us
    ppermute x5, starting transfers between devices, pair_swap(): return lax.ppermute(x, axis, route)  11.9 us
    pallas_call x1, Pallas kernels, feed_back(): call(functools.partial(field_kernel, parents, count), (rows // block,), [...  7.27 us
    pallas_call x1, Pallas kernels, feed_back(): call(seam_kernel, (seams,), [smem(), whole(2, seams, SUB, LANES), whole(s...  6.4 us
    pallas_call x1, Pallas kernels, feed_back(): call(functools.partial(partner_kernel, count), (rows // block,), [smem(),...  3.31 us
    another operation x1, loops' own time, shards(): return lax.cond(crossing <= SMALL_RUNG, run(SMALL_RUNG), run(most))  2.07 us
    pallas_call x1, Pallas kernels, feed_back(): call(functools.partial(rows_kernel, parents, count), (1,), [smem(), smem(...  1.74 us
    reduce_sum x1, other arithmetic, feed_back(): jnp.sum((own_map < window - 1).astype(jnp.int32), axis=1, keepdims=True)  1.57 us
  transfers between devices with their start and end apart: 5, of which 0 were waited for; matrix products, arithmetic and copies ran while one was open for 3% of the time, Pallas kernels for 45%

commit v1 on v0

v1 whole, which is shorter than its diff:
```python
import functools

import jax
import jax.numpy as jnp
from jax import lax
from jax.experimental import pallas as pl
from jax.experimental.pallas import tpu as pltpu
from jax.sharding import PartitionSpec as P

SMOOTH = 4
LANES = 128
SUB = 8
SLOT = 24
PER_TILE = 5
PER_SENT = 3
SMALL_RUNG = 1
ROW_BLOCK = 32
F32 = jnp.float32
BF16 = jnp.bfloat16
VMEM_MIB = 1 << 20


def pair_swap(x, axis, parity):
    route = []
    for low in range(parity, lax.axis_size(axis) - 1, 2):
        route += [(low, low + 1), (low + 1, low)]
    return lax.ppermute(x, axis, route)


def call(kernel, grid, in_specs, out_specs, out_shape, scratch=(), flops=1, limit=24):
    return pl.pallas_call(
        kernel,
        grid=grid,
        in_specs=in_specs,
        out_specs=out_specs,
        out_shape=out_shape,
        scratch_shapes=list(scratch),
        compiler_params=pltpu.CompilerParams(vmem_limit_bytes=limit * VMEM_MIB),
        cost_estimate=pl.CostEstimate(flops=flops, bytes_accessed=1 << 20, transcendentals=0),
    )


def smem():
    return pl.BlockSpec(memory_space=pltpu.SMEM)


def whole(*shape):
    return pl.BlockSpec(shape, lambda *_: (0,) * len(shape))


def deal_column(row, size):
    r = lax.broadcasted_iota(jnp.int32, (size, size), 0)
    c = lax.broadcasted_iota(jnp.int32, (size, size), 1)
    return jnp.sum(jnp.where(r == c, row, 0.0), axis=1, keepdims=True)


def share_columns(table, size, total):
    begins, inside, thick = (deal_column(table[i : i + 1, :size], size) for i in range(3))
    parent = lax.broadcasted_iota(jnp.int32, (size, LANES), 1).astype(F32)
    raw = jnp.where(parent == begins, inside * thick, 0.0)
    upper = jnp.minimum(begins + 1.0, total - 1.0)
    raw = raw + jnp.where(parent == upper, (1.0 - inside) * thick, 0.0)
    sums = jnp.where(parent < total, jnp.sum(raw, axis=0, keepdims=True), 1.0)
    normed = (raw / sums).astype(BF16).astype(F32)
    low = jnp.sum(jnp.where(parent == begins, normed, 0.0), axis=1, keepdims=True)
    high = jnp.sum(jnp.where(parent == begins + 1.0, normed, 0.0), axis=1, keepdims=True)
    return low, high


def remap_kernel(count, total, info, begins, table, child, par, mask, field, part, acc, low, high):
    children, parents = child.shape[0], field.shape[0]
    size, width = low.shape

    @pl.when(pl.program_id(0) == 0)
    def _():
        below, above = share_columns(table, size, total)
        low[...] = jnp.broadcast_to(below, low.shape)
        high[...] = jnp.broadcast_to(above, high.shape)

    slab = info[7]
    origin = slab * children
    trash = parents + count
    first = begins[origin] - slab * parents
    last = begins[origin + children - 1] - slab * parents

    def clear(p, carry):
        acc[p] = jnp.zeros(acc.shape[1:], F32)
        return carry

    lax.fori_loop(0, jnp.maximum(first, 0), clear, 0)
    untouched = jnp.where(slab == 0, last + 2, parents)
    end = parents + jnp.where(slab == 0, count, jnp.clip(first + count, 0, count))
    lax.fori_loop(untouched, end, clear, 0)

    def step(k, state):
        here, above = state
        level = begins[origin + k]
        rose = level != begins[jnp.maximum(origin + k - 1, 0)]
        value = child[k].astype(F32)
        here = jnp.where(rose, above, here) + low[pl.ds(origin + k, 1), :] * value
        above = jnp.where(rose, 0.0, above) + high[pl.ds(origin + k, 1), :] * value
        place = level - slab * parents
        place = jnp.where(place >= 0, place, parents + count + place)
        acc[jnp.clip(place, 0, trash)] = here
        return here, above

    zero = jnp.zeros(acc.shape[1:], F32)
    here, above = lax.fori_loop(0, children, step, (zero, zero), unroll=4)
    acc[jnp.where(slab == 0, jnp.clip(last + 1, 0, trash), trash)] = above
    fed = mask[...] != 0

    def blend(p, carry):
        field[p] = jnp.where(fed, acc[p], par[p].astype(F32)).astype(BF16)
        return carry

    lax.fori_loop(0, parents, blend, 0, unroll=5)

    def pass_on(j, carry):
        part[j] = acc[parents + j].astype(BF16)
        return carry

    lax.fori_loop(0, count, pass_on, 0)


def rows_kernel(count, info, field_t, field_b, mask_t, mask_b, part_t, part_b, even, odd, top, bot):
    parents = field_t.shape[0]
    row = lax.broadcasted_iota(jnp.int32, field_t.shape[1:], 0)
    flip = info[0] == 1
    fed_t, fed_b = mask_t[...] != 0, mask_b[...] != 0

    def copy(p, carry):
        top[p] = field_t[p].astype(F32)
        bot[p] = field_b[p].astype(F32)
        return carry

    lax.fori_loop(0, parents, copy, 0, unroll=9)

    def add_partner(j, carry):
        p = info[2] + j
        top[p] += jnp.where(fed_t, part_t[j].astype(F32), 0.0)
        bot[p] += jnp.where(fed_b, part_b[j].astype(F32), 0.0)
        return carry

    lax.fori_loop(0, count, add_partner, 0)
    for m in range(even.shape[0]):
        p, q = 2 * m, min(2 * m + 1, parents - 1)
        first = jnp.where(row < SMOOTH, top[p], pltpu.roll(top[q], SMOOTH, 0))
        last = jnp.where(row < SMOOTH, pltpu.roll(bot[p], SMOOTH, 0), bot[q])
        even[m] = jnp.where(flip, first, last).astype(BF16)
        odd[m] = jnp.where(flip, last, first).astype(BF16)


def edge_kernel(count, info, field, mask, part, fixed, edge, sent):
    parents = field.shape[0]
    fed = mask[...] != 0

    def fix(j, carry):
        value = field[info[2] + j].astype(F32) + jnp.where(fed, part[j].astype(F32), 0.0)
        fixed[j] = value.astype(BF16)
        return carry

    lax.fori_loop(0, count, fix, 0)

    def load(p):
        value = field[p].astype(F32)
        for start, near in ((0, p < count), (parents - count, p >= parents - count)):
            if near:
                mine = info[2] == start
                value = jnp.where(mine, fixed[p - start].astype(F32), value)
        return value

    edges = make_edges(parents, load)
    for t, tile in enumerate(edges):
        edge[t] = tile.astype(BF16)
    for t, tile in enumerate(make_sent(edges)):
        sent[t] = tile.astype(BF16)


def make_edges(parents, load):
    tiles = []
    for t in range(pl.cdiv(parents, PER_TILE)):
        tile = None
        for j in range(min(PER_TILE, parents - t * PER_TILE)):
            value = load(t * PER_TILE + j)
            lane = lax.broadcasted_iota(jnp.int32, (value.shape[0], LANES), 1)
            both = jnp.where(lane < LANES // 2, value[:, :LANES], value[:, -LANES:])
            both = pltpu.roll(both, (SLOT * j + 8) % LANES, 1)
            tile = both if tile is None else jnp.where(lane >= SLOT * j, both, tile)
        tiles.append(jnp.where(lane % SLOT < 8, tile, pltpu.roll(tile, 8, 1)))
    return tiles


def make_sent(edges):
    tiles = []
    for q in range(pl.cdiv(len(edges), PER_SENT)):
        tile = None
        for u, edge in enumerate(edges[q * PER_SENT : (q + 1) * PER_SENT]):
            lane = lax.broadcasted_iota(jnp.int32, edge.shape, 1) % SLOT - 8 * u
            last = pltpu.roll(edge, (8 * u - 4) % LANES, 1)
            first = pltpu.roll(edge, (8 * u - 12) % LANES, 1)
            both = jnp.where(lane < 4, last, first)
            tile = both if tile is None else jnp.where(lane >= 0, both, tile)
        tiles.append(tile)
    return tiles


def halo_kernel(parents, info, even, odd, sent_core, halo, edge, sent):
    flip = info[0] == 1
    row = lax.broadcasted_iota(jnp.int32, halo.shape[1:], 0)

    def load(p):
        a, b = even[p // 2].astype(F32), odd[p // 2].astype(F32)
        after, before = jnp.where(flip, b, a), jnp.where(flip, a, b)
        if p % 2 == 0:
            before = pltpu.roll(before, SMOOTH, 0)
        else:
            after = pltpu.roll(after, SMOOTH, 0)
        value = jnp.where(row < SMOOTH, after, before)
        halo[p] = value.astype(BF16)
        return value

    edges = make_edges(parents, load)
    for t, tile in enumerate(edges):
        edge[t] = tile.astype(BF16)
    rows = sent_core.shape[1]
    sent[:, :rows, :] = sent_core[...]
    for t, tile in enumerate(make_sent(edges)):
        sent[t, rows:, :] = tile.astype(BF16)


def row_sweep(values, side_sum, scales, keeps):
    count = len(values)
    before = pltpu.roll(values[-1], 1, 0)
    after = pltpu.roll(values[0], SUB - 1, 0)
    out = []
    for i, value in enumerate(values):
        up = values[i - 1] if i > 0 else before
        down = values[i + 1] if i < count - 1 else after
        out.append(keeps[i] * value + scales[i] * ((up + down) + side_sum(i, value)))
    return out


def row_flags(info, count, rows):
    sub = lax.broadcasted_iota(jnp.int32, (SUB, LANES), 0)
    flags = []
    for i in range(count):
        r = (SUB - 1) * count + i - rows
        if r < 0:
            flags.append(None)
            continue
        inside = info[4] if r < SMOOTH else info[3]
        flags.append(jnp.where(sub == SUB - 1, inside.astype(F32), 1.0))
    return flags


def smooth_kernel(count, info, coefs, field, fixed, halo, out, left, right, work, sides, near):
    levels, rows = field.shape[:2]
    deals = left.shape[1] // SUB
    flags = row_flags(info, deals, rows)
    flags = [None if f is None else jnp.concatenate([f, f], axis=1) for f in flags]
    base = pl.program_id(0) * levels

    @pl.when(pl.program_id(0) == 0)
    def _():
        r = lax.broadcasted_iota(jnp.int32, near.shape, 0)
        c = lax.broadcasted_iota(jnp.int32, near.shape, 1)
        near[...] = jnp.where(jnp.abs(r - c) == 1, 1.0, 0.0).astype(BF16)

    weights = []
    for p in range(levels):
        scale = coefs[base + p]
        keep = 1.0 - 4.0 * scale
        weights.append(
            (
                [scale if f is None else scale * f for f in flags],
                [keep if f is None else keep * f for f in flags],
            )
        )
        j = base + p - info[2]
        use_fixed = (j >= 0) & (j < count)
        j = jnp.clip(j, 0, count - 1)
        for ref, cut in ((left, slice(0, LANES)), (right, slice(LANES, 2 * LANES))):
            ref[p, :rows, :] = field[p, :, cut].astype(F32)

            @pl.when(use_fixed)
            def _():
                ref[p, :rows, :] = fixed[j, :, cut].astype(F32)

            ref[p, rows:, :] = halo[p, :, cut].astype(F32)
        for i in range(deals):
            part = slice(SUB * i, SUB * i + SUB)
            work[0, p, part, :LANES] = left[p, pl.ds(i, SUB, stride=deals), :]
            work[0, p, part, LANES:] = right[p, pl.ds(i, SUB, stride=deals), :]
    for s in range(SMOOTH):
        flat = work[s % 2].reshape(levels * deals * SUB, 2 * LANES).astype(BF16)
        side = jnp.dot(flat, near[...], preferred_element_type=F32)
        sides[...] = side.reshape(sides.shape)
        for p in range(levels):
            values = [work[s % 2, p, SUB * i : SUB * i + SUB, :] for i in range(deals)]
            values = row_sweep(
                values, lambda i, _: sides[p, SUB * i : SUB * i + SUB, :], *weights[p]
            )
            for i, value in enumerate(values):
                if s == SMOOTH - 1:
                    left[p, pl.ds(i, SUB, stride=deals), :] = value[:, :LANES]
                    right[p, pl.ds(i, SUB, stride=deals), :] = value[:, LANES:]
                else:
                    work[(s + 1) % 2, p, SUB * i : SUB * i + SUB, :] = value
    for p in range(levels):
        out[p, :, :LANES] = left[p, :rows, :].astype(BF16)
        out[p, :, LANES:] = right[p, :rows, :].astype(BF16)


def seam_kernel(info, coefs, even, odd, core, edge, main, out, tiles, work):
    total = tiles.shape[0]
    rows = core.shape[1]
    count = tiles.shape[1] // SUB
    step = pl.program_id(0)

    @pl.when(step == 0)
    def _():
        flip = info[1] == 1
        flags = row_flags(info, count, rows)
        slot = lax.broadcasted_iota(jnp.int32, tiles.shape[1:], 1) % SLOT
        for q in range(even.shape[0]):
            a, b = even[q].astype(F32), odd[q].astype(F32)
            after, before = jnp.where(flip, b, a), jnp.where(flip, a, b)
            for u in range(min(PER_SENT, total - q * PER_SENT)):
                t = q * PER_SENT + u
                own = jnp.concatenate([core[t].astype(F32), edge[t].astype(F32)], axis=0)
                right = pltpu.roll(after, (4 - 8 * u) % LANES, 1)
                left = pltpu.roll(before, (12 - 8 * u) % LANES, 1)
                tile = jnp.where(slot < 12, right, left)
                tiles[t] = jnp.where((slot >= 8) & (slot < 16), tile, own)
        for t in range(total):
            for i in range(count):
                work[0, t, i] = tiles[t, pl.ds(i, SUB, stride=count), :]
        for s in range(SMOOTH):
            for t in range(total):
                scale = coefs[0, t]
                keep = coefs[1, t]
                scales = [scale if f is None else scale * f for f in flags]
                keeps = [keep if f is None else keep * f for f in flags]
                values = [work[s % 2, t, i] for i in range(count)]
                new = row_sweep(
                    values,
                    lambda _, x: pltpu.roll(x, 1, 1) + pltpu.roll(x, LANES - 1, 1),
                    scales,
                    keeps,
                )
                for i in range(count):
                    if s < SMOOTH - 1:
                        work[(s + 1) % 2, t, i] = new[i]
                    else:
                        tiles[t, pl.ds(i, SUB, stride=count), :] = new[i]

    seam = tiles[step, :rows, :]
    lane = lax.broadcasted_iota(jnp.int32, seam.shape, 1)
    seam = jnp.where(lane % SLOT < 8, seam, pltpu.roll(seam, LANES - 8, 1))
    for j in range(main.shape[0]):
        first = last = pltpu.roll(seam, (120 - SLOT * j) % LANES, 1)
        a, b = main[j, :, :LANES].astype(F32), main[j, :, LANES:].astype(F32)
        out[j, :, :LANES] = jnp.where(lane < SMOOTH, first, a).astype(BF16)
        out[j, :, LANES:] = jnp.where(lane >= LANES - SMOOTH, last, b).astype(BF16)


def feed_back(count, child, parent, table, level_map, smooth_coef, mask):
    children, rows, columns = child.shape
    parents = parent.shape[0]
    total = parents * lax.axis_size("lev")
    size = level_map.shape[0]
    slab = lax.axis_index("lev")
    gx, gy = lax.axis_index("gx"), lax.axis_index("gy")
    info = jnp.stack(
        [
            gx % 2,
            gy % 2,
            jnp.where(slab == 0, parents - count, 0),
            (gx > 0).astype(jnp.int32),
            (gx < lax.axis_size("gx") - 1).astype(jnp.int32),
            (gy > 0).astype(jnp.int32),
            (gy < lax.axis_size("gy") - 1).astype(jnp.int32),
            slab,
        ]
    ).astype(jnp.int32)

    block = ROW_BLOCK
    field, part = call(
        functools.partial(remap_kernel, count, total),
        (rows // block,),
        [
            smem(), smem(), whole(*table.shape),
            pl.BlockSpec((children, block, columns), lambda i: (0, i, 0)),
            pl.BlockSpec((parents, block, columns), lambda i: (0, i, 0)),
            pl.BlockSpec((block, columns), lambda i: (i, 0)),
        ],
        [
            pl.BlockSpec((parents, block, columns), lambda i: (0, i, 0)),
            pl.BlockSpec((count, block, columns), lambda i: (0, i, 0)),
        ],
        [
            jax.ShapeDtypeStruct((parents, rows, columns), BF16),
            jax.ShapeDtypeStruct((count, rows, columns), BF16),
        ],
        [pltpu.VMEM((parents + count + 1, block, columns), F32)]
        + [pltpu.VMEM((size, columns), F32)] * 2,
    )(info, level_map, table, child, parent, mask)
    part = pair_swap(part, "lev", 0)

    ends = rows // SUB - 1

    def two(lead):
        return [
            pl.BlockSpec((lead, SUB, columns), lambda i: (0, 0, 0)),
            pl.BlockSpec((lead, SUB, columns), lambda i: (0, ends, 0)),
        ]

    packed = pl.cdiv(parents, 2)
    strip = jax.ShapeDtypeStruct((packed, SUB, columns), BF16)
    row_even, row_odd = call(
        functools.partial(rows_kernel, count),
        (1,),
        [
            smem(),
            *two(parents),
            pl.BlockSpec((SUB, columns), lambda i: (0, 0)),
            pl.BlockSpec((SUB, columns), lambda i: (ends, 0)),
            *two(count),
        ],
        [whole(packed, SUB, columns)] * 2,
        [strip, strip],
        [pltpu.VMEM((parents, SUB, columns), F32)] * 2,
    )(info, field, field, mask, mask, part, part)
    row_even = pair_swap(row_even, "gx", 0)
    row_odd = pair_swap(row_odd, "gx", 1)

    seams = pl.cdiv(parents, PER_TILE)
    sents = pl.cdiv(seams, PER_SENT)
    fixed, edge_core, sent_core = call(
        functools.partial(edge_kernel, count),
        (rows // block,),
        [
            smem(),
            pl.BlockSpec((parents, block, columns), lambda i: (0, i, 0)),
            pl.BlockSpec((block, columns), lambda i: (i, 0)),
            pl.BlockSpec((count, block, columns), lambda i: (0, i, 0)),
        ],
        [
            pl.BlockSpec((count, block, columns), lambda i: (0, i, 0)),
            pl.BlockSpec((seams, block, LANES), lambda i: (0, i, 0)),
            pl.BlockSpec((sents, block, LANES), lambda i: (0, i, 0)),
        ],
        [
            jax.ShapeDtypeStruct((count, rows, columns), BF16),
            jax.ShapeDtypeStruct((seams, rows, LANES), BF16),
            jax.ShapeDtypeStruct((sents, rows, LANES), BF16),
        ],
        flops=1 << 34,
    )(info, field, mask, part)

    extended = rows + SUB
    halo, edge_halo, sent = call(
        functools.partial(halo_kernel, parents),
        (1,),
        [smem(), whole(packed, SUB, columns), whole(packed, SUB, columns), whole(sents, rows, LANES)],
        [whole(parents, SUB, columns), whole(seams, SUB, LANES), whole(sents, extended, LANES)],
        [
            jax.ShapeDtypeStruct((parents, SUB, columns), BF16),
            jax.ShapeDtypeStruct((seams, SUB, LANES), BF16),
            jax.ShapeDtypeStruct((sents, extended, LANES), BF16),
        ],
    )(info, row_even, row_odd, sent_core)
    column_even = pair_swap(sent, "gy", 0)
    column_odd = pair_swap(sent, "gy", 1)

    group = PER_TILE
    main = call(
        functools.partial(smooth_kernel, count),
        (parents // group,),
        [
            smem(), smem(),
            pl.BlockSpec((group, rows, columns), lambda i: (i, 0, 0)),
            whole(count, rows, columns),
            pl.BlockSpec((group, SUB, columns), lambda i: (i, 0, 0)),
        ],
        pl.BlockSpec((group, rows, columns), lambda i: (i, 0, 0)),
        jax.ShapeDtypeStruct((parents, rows, columns), BF16),
        [pltpu.VMEM((group, extended, LANES), F32)] * 2
        + [
            pltpu.VMEM((2, group, extended, columns), F32),
            pltpu.VMEM((group, extended, columns), F32),
            pltpu.VMEM((columns, columns), BF16),
        ],
        flops=1 << 34,
    )(info, smooth_coef, field, fixed, halo)

    lane = jnp.arange(LANES, dtype=jnp.int32)
    place_in_slot = lane % SLOT
    inside = lane < SLOT * PER_TILE
    after = (place_in_slot >= 8) & (place_in_slot < 12)
    before = (place_in_slot >= 12) & (place_in_slot < 16)
    inside &= ~after | (gy < lax.axis_size("gy") - 1)
    inside &= ~before | (gy > 0)
    by_tile = jnp.repeat(smooth_coef.reshape(seams, PER_TILE), SLOT, axis=1)
    by_tile = jnp.pad(by_tile, ((0, 0), (0, LANES - SLOT * PER_TILE)))
    lane_coefs = jnp.where(inside, jnp.stack([by_tile, 1.0 - 4.0 * by_tile]), 0.0)
    lane_coefs = jnp.broadcast_to(lane_coefs[:, :, None, :], (2, seams, SUB, LANES))
    return call(
        seam_kernel,
        (seams,),
        [
            smem(),
            whole(2, seams, SUB, LANES),
            whole(sents, extended, LANES),
            whole(sents, extended, LANES),
            whole(seams, rows, LANES),
            whole(seams, SUB, LANES),
            pl.BlockSpec((group, rows, columns), lambda i: (i, 0, 0)),
        ],
        pl.BlockSpec((group, rows, columns), lambda i: (i, 0, 0)),
        jax.ShapeDtypeStruct((parents, rows, columns), BF16),
        [
            pltpu.VMEM((seams, extended, LANES), F32),
            pltpu.VMEM((2, seams, extended // SUB, SUB, LANES), F32),
        ],
    )(info, lane_coefs, column_even, column_odd, edge_core, edge_halo, main)


def shards(child_field, parent_old, level_map, intersection, thickness, smooth_coef, nest_mask):
    children, parents = child_field.shape[0], parent_old.shape[0]
    most = children - parents + 1
    crossing = jnp.maximum(level_map[children - 1] + 2 - parents, parents - level_map[children])
    table = jnp.stack([level_map.astype(F32), intersection, thickness])
    table = jnp.pad(table, ((0, SUB - 3), (0, -level_map.shape[0] % LANES)))

    def run(count):
        return lambda: feed_back(
            count, child_field, parent_old, table, level_map, smooth_coef, nest_mask
        )

    return lax.cond(crossing <= SMALL_RUNG, run(SMALL_RUNG), run(most))


def solution(mesh):
    in_specs = (P("lev", "gx", "gy"), P("lev", "gx", "gy"), P(), P(), P(), P("lev"), P("gx", "gy"))
    out_specs = P("lev", "gx", "gy")
    return jax.shard_map(shards, mesh=mesh, in_specs=in_specs, out_specs=out_specs, check_vma=False)
```

time: 67.4 us -> 48.1 us (0.71)
  the two profiles are of different devices: /device:TPU:49 before, /device:TPU:35 now
where the time goes in v1:
time: 48.1 us; the launch traced here: 47.8 us
  Pallas kernels  24.3 us (51%)
  starting transfers between devices  12.6 us (26%)
  waiting for transfers between devices  4.64 us (10%)
  local copies, waits for them, and re-layouts  3.34 us (7%)
  other arithmetic  1.42 us (3%)
  between operations  1.35 us (3%)
    ppermute x5, starting transfers between devices, pair_swap(): return lax.ppermute(x, axis, route)  12.6 us
    pallas_call x1, Pallas kernels, feed_back(): call(functools.partial(smooth_kernel, count), (parents // group,), [smem(...  9.42 us
    pallas_call x1, Pallas kernels, feed_back(): call(functools.partial(remap_kernel, count, total), (rows // block,), [sm...  6.61 us
    ppermute x5, waiting for transfers between devices, pair_swap(): return lax.ppermute(x, axis, route)  4.64 us
    pallas_call x1, Pallas kernels, feed_back(): call(seam_kernel, (seams,), [smem(), whole(2, seams, SUB, LANES), whole(s...  4.08 us
    pallas_call x1, Pallas kernels, feed_back(): call(functools.partial(edge_kernel, count), (rows // block,), [smem(), pl...  2.67 us
    unnamed x2, local copies, waits for them, and re-layouts  1.59 us
    slice x1, local copies, waits for them, and re-layouts, shards(): level_map[children]  1.4 us
  transfers between devices with their start and end apart: 5, of which 2 were waited for; matrix products, arithmetic and copies ran while one was open for 1% of the time, Pallas kernels for 25%

profile of v1, /device:TPU:35, one launch (start us, length us, event | category | flops | bytes accessed | tf_op | source)
XLA Modules:
  0.0 47.8 jit_solution(1872552120971465161)
XLA Ops:
  0.0 1.4 %fusion = (s32[1]{0:T(128)}, s32[1]{0:T(128)}) fusion(s32[136]{0:T(256)} %param.11), kind=kLoop, calls=%fused_computation.11 | loop fusion | bytes 16 | tf_op jit(solution)/shard_map/slice | solution.py:532
  2.7 0.7 %convert_element_type.24 = f32[136]{0:T(256)S(1)} convert(s32[136]{0:T(256)} %param.11) | non-fusion elementwise | flops 136 | bytes 1088 | tf_op jit(solution)/shard_map/convert_element_type | solution.py:533
  3.4 0.7 %pad_maximum_fusion = f32[3,136]{1,0:T(4,128)S(1)} fusion(f32[1,136]{1,0:T(1,128)} %bitcast.29, f32[1,136]{1,0:T(1,128)} %bitcast.30, f32[1,136]{1,0:T(1,128)S(1)} %bitcast.28), kind=kLoop, calls=%fused_computation.10 | loop fusion | flops 816 | bytes 3264 | tf_op jit(solution)/shard_map/stack | solution.py:533
  4.1 42.1 %conditional.1 = (bf16[45,128,256]{2,1,0:T(8,128)(2,1)S(1)}) conditional(s32[]{:T(128)} %bitcast.20, (f32[45]{0:T(128)}, s32[136]{0:T(256)}, f32[3,136]{1,0:T(4,128)S(1)}, bf16[68,128,256]{2,1,0:T(8,128)(2,1)}, bf16[45,128,256]{2,1,0:T(8,128)(2,1)}, /*index=5*/s32[128,256]{1,0:T(8,128)}, ()) %tuple.11, (f32[45]{0:T(128)}, s32[136]{0:T(256)}, ...), branch_computations={%region_0.1_spmd, %region_1.2_spmd} | conditional | flops 34359746560 | bytes 14836374 | solution.py:541
  4.2 0.1 stack.100.info
  4.3 0.0 copy-start.4
  4.3 0.0 copy-start.1
  4.3 6.6 %branch_1_fun.6 = (bf16[45,128,256]{2,1,0:T(8,128)(2,1)S(1)}, bf16[1,128,256]{2,1,0:T(8,128)(2,1)S(1)}) custom-call(s32[8]{0:T(128)S(1)} %stack.100.info, s32[136]{0:T(256)} %get-tuple-element.49.begins, f32[8,256]{1,0:T(8,128)S(1)} %pad.13.table, bf16[68,128,256]{2,1,0:T(8,128)(2,1)} %get-tuple-element.80.child, ...), custom_call_target="tpu_custom_call" | custom-call | flops 1 | bytes 1048576 | tf_op jit(solution)/shard_map/cond/branch_1_fun/pallas_call | solution.py:388
  10.9 1.4 %collective-permute-start.5 = (bf16[1,128,256]{2,1,0:T(8,128)(2,1)S(1)}, bf16[1,128,256]{2,1,0:T(8,128)(2,1)S(1)}, u32[]{:S(2)}, u32[]{:S(2)}) collective-permute-start(bf16[1,128,256]{2,1,0:T(8,128)(2,1)S(1)} %get-tuple-element.55), channel_id=1, source_target_pairs={{0,1},{1,0},{2,3},{3,2},{4,5},{5,4},{6,7},{7,6},{8,9},{9,8},{10,11... | collective-permute-start | bytes 196616 | tf_op jit(solution)/shard_map/cond/branch_1_fun/ppermute | solution.py:27
  12.3 0.0 copy-done.4
  12.3 0.1 reshape.53
  12.4 0.1 broadcast_in_dim.29
  12.5 0.1 reshape.54
  12.6 1.5 %collective-permute-done.5.part_t.part_b.part = bf16[1,128,256]{2,1,0:T(8,128)(2,1)S(1)} collective-permute-done((bf16[1,128,256]{2,1,0:T(8,128)(2,1)S(1)}, bf16[1,128,256]{2,1,0:T(8,128)(2,1)S(1)}, u32[]{:S(2)}, u32[]{:S(2)}) %collective-permute-start.5) | collective-permute-done | bytes 65568 | tf_op jit(solution)/shard_map/cond/branch_1_fun/ppermute | solution.py:27
  14.1 0.0 copy-done.1
  14.1 0.7 %branch_1_fun.7 = (bf16[23,8,256]{2,1,0:T(8,128)(2,1)S(1)}, bf16[23,8,256]{2,1,0:T(8,128)(2,1)S(1)}) custom-call(s32[8]{0:T(128)S(1)} %stack.100.info, bf16[45,128,256]{2,1,0:T(8,128)(2,1)S(1)} %get-tuple-element.54.field_t.field_b.field, bf16[45,128,256]{2,1,0:T(8,128)(2,1)S(1)} %get-tuple-element.54.field_t.field_b.field, s32[128,256]{1,0:T(8,128)S(1)} %copy-done.1, ...), custom_call_target="tpu_custom_call" | custom-call | flops 1 | bytes 1048576 | tf_op jit(solution)/shard_map/cond/branch_1_fun/pallas_call | solution.py:420
  14.8 3.0 %collective-permute-start.6 = (bf16[23,8,256]{2,1,0:T(8,128)(2,1)S(1)}, bf16[23,8,256]{2,1,0:T(8,128)(2,1)S(1)}, u32[]{:S(2)}, u32[]{:S(2)}) collective-permute-start(bf16[23,8,256]{2,1,0:T(8,128)(2,1)S(1)} %get-tuple-element.56), channel_id=1, source_target_pairs={{0,16},{16,0},{32,48},{48,32},{64,80},{80,64},{96,112},{112,96},{1... | collective-permute-start | bytes 282632 | tf_op jit(solution)/shard_map/cond/branch_1_fun/ppermute | solution.py:27
  17.8 1.9 %collective-permute-start.7 = (bf16[23,8,256]{2,1,0:T(8,128)(2,1)S(1)}, bf16[23,8,256]{2,1,0:T(8,128)(2,1)S(1)}, u32[]{:S(2)}, u32[]{:S(2)}) collective-permute-start(bf16[23,8,256]{2,1,0:T(8,128)(2,1)S(1)} %get-tuple-element.57), channel_id=1, source_target_pairs={{16,32},{32,16},{48,64},{64,48},{80,96},{96,80},{17,33},{33,17},{4... | collective-permute-start | bytes 282632 | tf_op jit(solution)/shard_map/cond/branch_1_fun/ppermute | solution.py:27
  19.7 2.7 %branch_1_fun.8 = (bf16[1,128,256]{2,1,0:T(8,128)(2,1)S(1)}, bf16[9,128,128]{2,1,0:T(8,128)(2,1)S(1)}, bf16[3,128,128]{2,1,0:T(8,128)(2,1)S(1)}) custom-call(s32[8]{0:T(128)S(1)} %stack.100.info, bf16[45,128,256]{2,1,0:T(8,128)(2,1)S(1)} %get-tuple-element.54.field_t.field_b.field, s32[128,256]{1,0:T(8,128)S(1)} %copy-done.1, ...), custom_call_target="tpu_custom_call" | custom-call | flops 17179869184 | bytes 1048576 | tf_op jit(solution)/shard_map/cond/branch_1_fun/pallas_call | solution.py:439
  22.4 0.0 collective-permute-done.6.even
  22.4 3.1 %collective-permute-done.7.odd = bf16[23,8,256]{2,1,0:T(8,128)(2,1)S(1)} collective-permute-done((bf16[23,8,256]{2,1,0:T(8,128)(2,1)S(1)}, bf16[23,8,256]{2,1,0:T(8,128)(2,1)S(1)}, u32[]{:S(2)}, u32[]{:S(2)}) %collective-permute-start.7) | collective-permute-done | bytes 94240 | tf_op jit(solution)/shard_map/cond/branch_1_fun/ppermute | solution.py:27
  25.5 0.8 %branch_1_fun.9 = (bf16[45,8,256]{2,1,0:T(8,128)(2,1)S(1)}, bf16[9,8,128]{2,1,0:T(8,128)(2,1)S(1)}, bf16[3,136,128]{2,1,0:T(8,128)(2,1)S(1)}) custom-call(s32[8]{0:T(128)S(1)} %stack.100.info, bf16[23,8,256]{2,1,0:T(8,128)(2,1)S(1)} %collective-permute-done.6.even, bf16[23,8,256]{2,1,0:T(8,128)(2,1)S(1)} %collective-permute-done.7.odd, ...), custom_call_target="tpu_custom_call" | custom-call | flops 1 | bytes 1048576 | tf_op jit(solution)/shard_map/cond/branch_1_fun/pallas_call | solution.py:462
  26.3 3.3 %collective-permute-start.8 = (bf16[3,136,128]{2,1,0:T(8,128)(2,1)S(1)}, bf16[3,136,128]{2,1,0:T(8,128)(2,1)S(1)}, u32[]{:S(2)}, u32[]{:S(2)}) collective-permute-start(bf16[3,136,128]{2,1,0:T(8,128)(2,1)S(1)} %get-tuple-element.59), channel_id=1, source_target_pairs={{0,2},{2,0},{4,6},{6,4},{8,10},{10,8},{12,14},{14,12},{1,3},{3,1},... | collective-permute-start | bytes 313352 | tf_op jit(solution)/shard_map/cond/branch_1_fun/ppermute | solution.py:27
  29.6 3.0 %collective-permute-start.9 = (bf16[3,136,128]{2,1,0:T(8,128)(2,1)S(1)}, bf16[3,136,128]{2,1,0:T(8,128)(2,1)S(1)}, u32[]{:S(2)}, u32[]{:S(2)}) collective-permute-start(bf16[3,136,128]{2,1,0:T(8,128)(2,1)S(1)} %get-tuple-element.59), channel_id=1, source_target_pairs={{2,4},{4,2},{6,8},{8,6},{10,12},{12,10},{3,5},{5,3},{7,9},{9,7},{1... | collective-permute-start | bytes 313352 | tf_op jit(solution)/shard_map/cond/branch_1_fun/ppermute | solution.py:27
  32.7 9.4 %branch_1_fun.10.main = bf16[45,128,256]{2,1,0:T(8,128)(2,1)S(1)} custom-call(s32[8]{0:T(128)S(1)} %stack.100.info, f32[45]{0:T(128)S(1)} %copy-done.4, bf16[45,128,256]{2,1,0:T(8,128)(2,1)S(1)} %get-tuple-element.54.field_t.field_b.field, bf16[1,128,256]{2,1,0:T(8,128)(2,1)S(1)} %get-tuple-element.62.fixed, bf16[45,8,256]{2,1,0:T(8,128)(2,1)S(1)} %get-tuple-element.63.halo), custom_call_target="tpu_custom_call" | custom-call | flops 17179869184 | bytes 1048576 | tf_op jit(solution)/shard_map/cond/branch_1_fun/pallas_call | solution.py:477
  42.1 0.0 collective-permute-done.8.even
  42.1 0.0 collective-permute-done.9.odd
  42.1 4.1 %branch_1_fun.11 = bf16[45,128,256]{2,1,0:T(8,128)(2,1)S(1)} custom-call(s32[8]{0:T(128)S(1)} %stack.100.info, f32[2,9,8,128]{3,2,1,0:T(8,128)S(1)} %broadcast_in_dim.31.coefs, bf16[3,136,128]{2,1,0:T(8,128)(2,1)S(1)} %collective-permute-done.8.even, bf16[3,136,128]{2,1,0:T(8,128)(2,1)S(1)} %collective-permute-done.9.odd, ...), custom_call_target="tpu_custom_call" | custom-call | flops 1 | bytes 1048576 | tf_op jit(solution)/shard_map/cond/branch_1_fun/pallas_call | solution.py:508
  46.2 0.0 copy-start.2
  46.2 1.6 %copy-done.2 = bf16[45,128,256]{2,1,0:T(8,128)(2,1)} copy-done((bf16[45,128,256]{2,1,0:T(8,128)(2,1)}, bf16[45,128,256]{2,1,0:T(8,128)(2,1)S(1)}, u32[]{:S(2)}) %copy-start.2) | copy-done | bytes 2949144
  (5 shorter events, 0.0 us)
Async XLA Ops:
  4.3 8.0 %copy-start.4 = (f32[45]{0:T(128)S(1)}, f32[45]{0:T(128)}, u32[]{:S(2)}) copy-start(f32[45]{0:T(128)} %get-tuple-element.78.coefs) | copy-start | bytes 544 | tf_op jit(solution)/shard_map/cond
  4.3 9.8 %copy-start.1 = (s32[128,256]{1,0:T(8,128)S(1)}, s32[128,256]{1,0:T(8,128)}, u32[]{:S(2)}) copy-start(s32[128,256]{1,0:T(8,128)} %get-tuple-element.84.mask.mask_t.mask_b) | copy-start | bytes 393220 | tf_op jit(solution)/shard_map/cond
  10.9 3.2 %collective-permute-start.5 = (bf16[1,128,256]{2,1,0:T(8,128)(2,1)S(1)}, bf16[1,128,256]{2,1,0:T(8,128)(2,1)S(1)}, u32[]{:S(2)}, u32[]{:S(2)}) collective-permute-start(bf16[1,128,256]{2,1,0:T(8,128)(2,1)S(1)} %get-tuple-element.55), channel_id=1, source_target_pairs={{0,1},{1,0},{2,3},{3,2},{4,5},{5,4},{6,7},{7,6},{8,9},{9,8},{10,11... | collective-permute-start | bytes 196616 | tf_op jit(solution)/shard_map/cond/branch_1_fun/ppermute | solution.py:27
  14.8 7.6 %collective-permute-start.6 = (bf16[23,8,256]{2,1,0:T(8,128)(2,1)S(1)}, bf16[23,8,256]{2,1,0:T(8,128)(2,1)S(1)}, u32[]{:S(2)}, u32[]{:S(2)}) collective-permute-start(bf16[23,8,256]{2,1,0:T(8,128)(2,1)S(1)} %get-tuple-element.56), channel_id=1, source_target_pairs={{0,16},{16,0},{32,48},{48,32},{64,80},{80,64},{96,112},{112,96},{1... | collective-permute-start | bytes 282632 | tf_op jit(solution)/shard_map/cond/branch_1_fun/ppermute | solution.py:27
  17.8 7.7 %collective-permute-start.7 = (bf16[23,8,256]{2,1,0:T(8,128)(2,1)S(1)}, bf16[23,8,256]{2,1,0:T(8,128)(2,1)S(1)}, u32[]{:S(2)}, u32[]{:S(2)}) collective-permute-start(bf16[23,8,256]{2,1,0:T(8,128)(2,1)S(1)} %get-tuple-element.57), channel_id=1, source_target_pairs={{16,32},{32,16},{48,64},{64,48},{80,96},{96,80},{17,33},{33,17},{4... | collective-permute-start | bytes 282632 | tf_op jit(solution)/shard_map/cond/branch_1_fun/ppermute | solution.py:27
  26.3 15.8 %collective-permute-start.8 = (bf16[3,136,128]{2,1,0:T(8,128)(2,1)S(1)}, bf16[3,136,128]{2,1,0:T(8,128)(2,1)S(1)}, u32[]{:S(2)}, u32[]{:S(2)}) collective-permute-start(bf16[3,136,128]{2,1,0:T(8,128)(2,1)S(1)} %get-tuple-element.59), channel_id=1, source_target_pairs={{0,2},{2,0},{4,6},{6,4},{8,10},{10,8},{12,14},{14,12},{1,3},{3,1},... | collective-permute-start | bytes 313352 | tf_op jit(solution)/shard_map/cond/branch_1_fun/ppermute | solution.py:27
  29.6 12.5 %collective-permute-start.9 = (bf16[3,136,128]{2,1,0:T(8,128)(2,1)S(1)}, bf16[3,136,128]{2,1,0:T(8,128)(2,1)S(1)}, u32[]{:S(2)}, u32[]{:S(2)}) collective-permute-start(bf16[3,136,128]{2,1,0:T(8,128)(2,1)S(1)} %get-tuple-element.59), channel_id=1, source_target_pairs={{2,4},{4,2},{6,8},{8,6},{10,12},{12,10},{3,5},{5,3},{7,9},{9,7},{1... | collective-permute-start | bytes 313352 | tf_op jit(solution)/shard_map/cond/branch_1_fun/ppermute | solution.py:27
  46.2 1.6 %copy-start.2 = (bf16[45,128,256]{2,1,0:T(8,128)(2,1)}, bf16[45,128,256]{2,1,0:T(8,128)(2,1)S(1)}, u32[]{:S(2)}) copy-start(bf16[45,128,256]{2,1,0:T(8,128)(2,1)S(1)} %get-tuple-element.111) | copy-start | bytes 8847364

commit v2 on v1

--- a/solution.py
+++ b/solution.py
@@ -54,8 +54,9 @@
     return jnp.sum(jnp.where(r == c, row, 0.0), axis=1, keepdims=True)
 
 
-def share_columns(table, size, total):
-    begins, inside, thick = (deal_column(table[i : i + 1, :size], size) for i in range(3))
+def share_columns(rows, size, total):
+    rows = [row[...].astype(F32).reshape(1, size) for row in rows]
+    begins, inside, thick = (deal_column(row, size) for row in rows)
     parent = lax.broadcasted_iota(jnp.int32, (size, LANES), 1).astype(F32)
     raw = jnp.where(parent == begins, inside * thick, 0.0)
     upper = jnp.minimum(begins + 1.0, total - 1.0)
@@ -67,13 +68,15 @@
     return low, high
 
 
-def remap_kernel(count, total, info, begins, table, child, par, mask, field, part, acc, low, high):
-    children, parents = child.shape[0], field.shape[0]
+def remap_kernel(
+    count, total, info, begins, levels, inside, thick, child, own, part, acc, low, high
+):
+    children, parents = child.shape[0], own.shape[0]
     size, width = low.shape
 
     @pl.when(pl.program_id(0) == 0)
     def _():
-        below, above = share_columns(table, size, total)
+        below, above = share_columns((levels, inside, thick), size, total)
         low[...] = jnp.broadcast_to(below, low.shape)
         high[...] = jnp.broadcast_to(above, high.shape)
 
@@ -107,19 +110,39 @@
     zero = jnp.zeros(acc.shape[1:], F32)
     here, above = lax.fori_loop(0, children, step, (zero, zero), unroll=4)
     acc[jnp.where(slab == 0, jnp.clip(last + 1, 0, trash), trash)] = above
-    fed = mask[...] != 0
-
-    def blend(p, carry):
-        field[p] = jnp.where(fed, acc[p], par[p].astype(F32)).astype(BF16)
+
+    def keep(p, carry):
+        own[p] = acc[p].astype(BF16)
         return carry
 
-    lax.fori_loop(0, parents, blend, 0, unroll=5)
+    lax.fori_loop(0, parents, keep, 0, unroll=5)
 
     def pass_on(j, carry):
         part[j] = acc[parents + j].astype(BF16)
         return carry
 
     lax.fori_loop(0, count, pass_on, 0)
+
+
+def blend_kernel(group, own, par, mask, field, old, sems):
+    steps = own.shape[0] // group
+
+    def copy(i):
+        levels = pl.ds(i * group, group)
+        return pltpu.make_async_copy(par.at[levels], old.at[levels], sems.at[i])
+
+    for i in range(steps):
+        copy(i).start()
+    fed = mask[...] != 0
+
+    def step(i, carry):
+        copy(i).wait()
+        for j in range(group):
+            p = i * group + j
+            field[p] = jnp.where(fed, own[p].astype(F32), old[p].astype(F32)).astype(BF16)
+        return carry
+
+    lax.fori_loop(0, steps, step, 0)
 
 
 def rows_kernel(count, info, field_t, field_b, mask_t, mask_b, part_t, part_b, even, odd, top, bot):
@@ -311,7 +334,7 @@
         out[p, :, LANES:] = right[p, :rows, :].astype(BF16)
 
 
-def seam_kernel(info, coefs, even, odd, core, edge, main, out, tiles, work):
+def seam_kernel(info, coefs, even, odd, core, edge, main, out, tiles, work, done, sems):
     total = tiles.shape[0]
     rows = core.shape[1]
     count = tiles.shape[1] // SUB
@@ -357,42 +380,55 @@
     seam = tiles[step, :rows, :]
     lane = lax.broadcasted_iota(jnp.int32, seam.shape, 1)
     seam = jnp.where(lane % SLOT < 8, seam, pltpu.roll(seam, LANES - 8, 1))
-    for j in range(main.shape[0]):
-        first = last = pltpu.roll(seam, (120 - SLOT * j) % LANES, 1)
+    group = main.shape[0]
+    for j in range(group):
+        both = pltpu.roll(seam, (120 - SLOT * j) % LANES, 1)
         a, b = main[j, :, :LANES].astype(F32), main[j, :, LANES:].astype(F32)
-        out[j, :, :LANES] = jnp.where(lane < SMOOTH, first, a).astype(BF16)
-        out[j, :, LANES:] = jnp.where(lane >= LANES - SMOOTH, last, b).astype(BF16)
-
-
-def feed_back(count, child, parent, table, level_map, smooth_coef, mask):
+        p = step * group + j
+        done[p, :, :LANES] = jnp.where(lane < SMOOTH, both, a).astype(BF16)
+        done[p, :, LANES:] = jnp.where(lane >= LANES - SMOOTH, both, b).astype(BF16)
+
+    def copy(i):
+        levels = pl.ds(i * group, group)
+        return pltpu.make_async_copy(done.at[levels], out.at[levels], sems.at[i])
+
+    copy(step).start()
+
+    @pl.when(step == total - 1)
+    def _():
+        for i in range(total):
+            copy(i).wait()
+
+
+def device_facts(start):
+    slab, gx, gy = lax.axis_index("lev"), lax.axis_index("gx"), lax.axis_index("gy")
+    facts = [
+        gx % 2,
+        gy % 2,
+        start,
+        gx > 0,
+        gx < lax.axis_size("gx") - 1,
+        gy > 0,
+        gy < lax.axis_size("gy") - 1,
+        slab,
+    ]
+    return jnp.stack([jnp.asarray(fact, jnp.int32) for fact in facts])
+
+
+def feed_back(count, child, parent, inside, thick, level_map, smooth_coef, mask):
     children, rows, columns = child.shape
     parents = parent.shape[0]
     total = parents * lax.axis_size("lev")
     size = level_map.shape[0]
     slab = lax.axis_index("lev")
-    gx, gy = lax.axis_index("gx"), lax.axis_index("gy")
-    info = jnp.stack(
-        [
-            gx % 2,
-            gy % 2,
-            jnp.where(slab == 0, parents - count, 0),
-            (gx > 0).astype(jnp.int32),
-            (gx < lax.axis_size("gx") - 1).astype(jnp.int32),
-            (gy > 0).astype(jnp.int32),
-            (gy < lax.axis_size("gy") - 1).astype(jnp.int32),
-            slab,
-        ]
-    ).astype(jnp.int32)
-
+    info = device_facts(jnp.where(slab == 0, parents - count, 0))
     block = ROW_BLOCK
-    field, part = call(
+    own, part = call(
         functools.partial(remap_kernel, count, total),
         (rows // block,),
         [
-            smem(), smem(), whole(*table.shape),
+            smem(), smem(), whole(size), whole(size), whole(size),
             pl.BlockSpec((children, block, columns), lambda i: (0, i, 0)),
-            pl.BlockSpec((parents, block, columns), lambda i: (0, i, 0)),
-            pl.BlockSpec((block, columns), lambda i: (i, 0)),
         ],
         [
             pl.BlockSpec((parents, block, columns), lambda i: (0, i, 0)),
@@ -404,8 +440,21 @@
         ],
         [pltpu.VMEM((parents + count + 1, block, columns), F32)]
         + [pltpu.VMEM((size, columns), F32)] * 2,
-    )(info, level_map, table, child, parent, mask)
+    )(info, level_map, level_map, inside, thick, child)
     part = pair_swap(part, "lev", 0)
+    group = PER_TILE
+    field = call(
+        functools.partial(blend_kernel, group),
+        (1,),
+        [whole(parents, rows, columns), pl.BlockSpec(memory_space=pltpu.HBM), whole(rows, columns)],
+        whole(parents, rows, columns),
+        jax.ShapeDtypeStruct((parents, rows, columns), BF16),
+        [
+            pltpu.VMEM((parents, rows, columns), BF16),
+            pltpu.SemaphoreType.DMA((parents // group,)),
+        ],
+        flops=1 << 34,
+    )(own, parent, mask)
 
     ends = rows // SUB - 1
 
@@ -494,6 +543,14 @@
         flops=1 << 34,
     )(info, smooth_coef, field, fixed, halo)
 
+    return finish(info, smooth_coef, column_even, column_odd, edge_core, edge_halo, main)
+
+
+def finish(info, smooth_coef, column_even, column_odd, edge_core, edge_halo, main):
+    parents, rows, columns = main.shape
+    seams, extended = edge_core.shape[0], column_even.shape[1]
+    sents, group = column_even.shape[0], PER_TILE
+    gy = lax.axis_index("gy")
     lane = jnp.arange(LANES, dtype=jnp.int32)
     place_in_slot = lane % SLOT
     inside = lane < SLOT * PER_TILE
@@ -517,11 +574,13 @@
             whole(seams, SUB, LANES),
             pl.BlockSpec((group, rows, columns), lambda i: (i, 0, 0)),
         ],
-        pl.BlockSpec((group, rows, columns), lambda i: (i, 0, 0)),
-        jax.ShapeDtypeStruct((parents, rows, columns), BF16),
+        pl.BlockSpec(memory_space=pltpu.HBM),
+        pltpu.HBM((parents, rows, columns), BF16),
         [
             pltpu.VMEM((seams, extended, LANES), F32),
             pltpu.VMEM((2, seams, extended // SUB, SUB, LANES), F32),
+            pltpu.VMEM((parents, rows, columns), BF16),
+            pltpu.SemaphoreType.DMA((seams,)),
         ],
     )(info, lane_coefs, column_even, column_odd, edge_core, edge_halo, main)
 
@@ -529,13 +588,12 @@
 def shards(child_field, parent_old, level_map, intersection, thickness, smooth_coef, nest_mask):
     children, parents = child_field.shape[0], parent_old.shape[0]
     most = children - parents + 1
-    crossing = jnp.maximum(level_map[children - 1] + 2 - parents, parents - level_map[children])
-    table = jnp.stack([level_map.astype(F32), intersection, thickness])
-    table = jnp.pad(table, ((0, SUB - 3), (0, -level_map.shape[0] % LANES)))
+    ends = level_map[children - 1 : children + 1]
+    crossing = jnp.max(ends * jnp.array([1, -1]) + jnp.array([2 - parents, parents]))
 
     def run(count):
         return lambda: feed_back(
-            count, child_field, parent_old, table, level_map, smooth_coef, nest_mask
+            count, child_field, parent_old, intersection, thickness, level_map, smooth_coef, nest_mask
         )
 
     return lax.cond(crossing <= SMALL_RUNG, run(SMALL_RUNG), run(most))

time: 48.1 us -> 44.2 us (0.919)
  local copies, waits for them, and re-layouts: 3.34 us -> 0.33 us
  Pallas kernels: 24.3 us -> 26 us
  waiting for transfers between devices: 4.64 us -> 3.12 us
  between operations: 1.35 us -> 0.65 us
    pallas_call x1 -> x2, Pallas kernels: 4.08 us -> 6.88 us  [the longest x1 4.94 us: finish(): call(seam_kernel, (seams,), [smem(), whole(2, seams, SUB, LANES), whole(s...]
    unnamed x2 -> x0, local copies, waits for them, and re-layouts: 1.59 us -> none
    ppermute x5, waiting for transfers between devices: 4.64 us -> 3.12 us  [pair_swap(): return lax.ppermute(x, axis, route)]
    reduce_max x0 -> x1, other arithmetic: none -> 1.42 us  [shards(): jnp.max(ends * jnp.array([1, -1]) + jnp.array([2 - parents, parents]))]
    slice x1 -> x0, local copies, waits for them, and re-layouts: 1.4 us -> none  [shards(): level_map[children]]
    pallas_call x1, Pallas kernels: 6.61 us -> 5.57 us  [feed_back(): call(functools.partial(remap_kernel, count, total), (rows // block,), [sm...]
    another operation x2 -> x1, other arithmetic: 0.72 us -> 0.01 us  [finish(): jnp.stack([by_tile, 1.0 - 4.0 * by_tile])]
    convert_element_type x1 -> x0, other arithmetic: 0.68 us -> none  [shards(): table = jnp.stack([level_map.astype(F32), intersection, thickness])]
  transfers between devices with their start and end apart: 5 -> 5, of which waited for: 2 -> 1; matrix products, arithmetic and copies ran while one was open for 1% -> 1% of each run, Pallas kernels for 25% -> 32%
where the time goes in v2:
time: 44.2 us; the launch traced here: 44 us
  Pallas kernels  26 us (59%)
  starting transfers between devices  12.2 us (28%)
  waiting for transfers between devices  3.12 us (7%)
  other arithmetic  1.45 us (3%)
  between operations  0.65 us (1%)
    ppermute x5, starting transfers between devices, pair_swap(): return lax.ppermute(x, axis, route)  12.2 us
    pallas_call x1, Pallas kernels, feed_back(): call(functools.partial(smooth_kernel, count), (parents // group,), [smem(...  9.41 us
    pallas_call x1, Pallas kernels, feed_back(): call(functools.partial(remap_kernel, count, total), (rows // block,), [sm...  5.57 us
    pallas_call x1, Pallas kernels, finish(): call(seam_kernel, (seams,), [smem(), whole(2, seams, SUB, LANES), whole(s...  4.94 us
    ppermute x5, waiting for transfers between devices, pair_swap(): return lax.ppermute(x, axis, route)  3.12 us
    pallas_call x1, Pallas kernels, feed_back(): call(functools.partial(edge_kernel, count), (rows // block,), [smem(), pl...  2.67 us
    pallas_call x1, Pallas kernels, feed_back(): call(functools.partial(blend_kernel, group), (1,), [whole(parents, rows,...  1.94 us
    reduce_max x1, other arithmetic, shards(): jnp.max(ends * jnp.array([1, -1]) + jnp.array([2 - parents, parents]))  1.42 us
  transfers between devices with their start and end apart: 5, of which 1 were waited for; matrix products, arithmetic and copies ran while one was open for 1% of the time, Pallas kernels for 32%

profile of v2, /device:TPU:35, one launch (start us, length us, event | category | flops | bytes accessed | tf_op | source)
XLA Modules:
  0.0 44.0 jit_solution(1363061298812465727)
XLA Ops:
  0.0 1.4 %add_reduce_fusion = s32[]{:T(128)} fusion(s32[2]{0:T(128)} %constant.124.clone, s32[2]{0:T(128)} %constant.123.clone, s32[136]{0:T(256)} %param.13), kind=kLoop, calls=%fused_computation.10 | loop fusion | flops 5 | bytes 28 | tf_op jit(solution)/shard_map/reduce_max | solution.py:592
  2.1 41.9 %conditional.1 = (bf16[45,128,256]{2,1,0:T(8,128)(2,1)}) conditional(s32[]{:T(128)} %convert_element_type.4, (f32[45]{0:T(128)}, s32[136]{0:T(256)}, f32[136]{0:T(256)}, f32[136]{0:T(256)}, bf16[68,128,256]{2,1,0:T(8,128)(2,1)}, /*index=5*/bf16[45,128,256]{2,1,0:T(8,128)(2,1)}, s32[128,256]{1,0:T(8,128)}) %tuple.11, (f32[45]{0:T(128)}, s32[136]{0:T(256)}, ...), branch_computations={%region_1.2_spmd, %region_2.3_spmd} | conditional | flops 51539615744 | bytes 39468136 | solution.py:599
  2.1 0.0 copy-start.5
  2.1 0.0 copy-start.3
  2.1 0.1 stack.92.info
  2.2 5.6 %branch_1_fun.7 = (bf16[45,128,256]{2,1,0:T(8,128)(2,1)S(1)}, bf16[1,128,256]{2,1,0:T(8,128)(2,1)S(1)}) custom-call(s32[8]{0:T(128)S(1)} %stack.92.info, s32[136]{0:T(256)} %get-tuple-element.54.begins.levels, s32[136]{0:T(256)} %get-tuple-element.54.begins.levels, f32[136]{0:T(256)} %get-tuple-element.55.inside, f32[136]{0:T(256)} %get-tuple-element.56.thick, ...), custom_call_target="tpu_custom_call" | custom-call | flops 1 | bytes 1048576 | tf_op jit(solution)/shard_map/cond/branch_1_fun/pallas_call | solution.py:426
  7.8 1.4 %collective-permute-start.5 = (bf16[1,128,256]{2,1,0:T(8,128)(2,1)S(1)}, bf16[1,128,256]{2,1,0:T(8,128)(2,1)S(1)}, u32[]{:S(2)}, u32[]{:S(2)}) collective-permute-start(bf16[1,128,256]{2,1,0:T(8,128)(2,1)S(1)} %get-tuple-element.61), channel_id=1, source_target_pairs={{0,1},{1,0},{2,3},{3,2},{4,5},{5,4},{6,7},{7,6},{8,9},{9,8},{10,11... | collective-permute-start | bytes 196616 | tf_op jit(solution)/shard_map/cond/branch_1_fun/ppermute | solution.py:27
  9.2 0.0 copy-done.5
  9.2 0.1 reshape.44
  9.3 0.1 broadcast_in_dim.29
  9.4 0.1 reshape.45
  9.5 0.0 copy-done.3
  9.5 1.9 %branch_1_fun.8.field_t.field_b.field = bf16[45,128,256]{2,1,0:T(8,128)(2,1)S(1)} custom-call(bf16[45,128,256]{2,1,0:T(8,128)(2,1)S(1)} %get-tuple-element.58.own, bf16[45,128,256]{2,1,0:T(8,128)(2,1)} %get-tuple-element.59.par, s32[128,256]{1,0:T(8,128)S(1)} %copy-done.3), custom_call_target="tpu_custom_call" | custom-call | flops 17179869184 | bytes 1048576 | tf_op jit(solution)/shard_map/cond/branch_1_fun/pallas_call | solution.py:446
  11.4 0.0 collective-permute-done.5.part_t.part_b.part
  11.4 0.7 %branch_1_fun.9 = (bf16[23,8,256]{2,1,0:T(8,128)(2,1)S(1)}, bf16[23,8,256]{2,1,0:T(8,128)(2,1)S(1)}) custom-call(s32[8]{0:T(128)S(1)} %stack.92.info, bf16[45,128,256]{2,1,0:T(8,128)(2,1)S(1)} %branch_1_fun.8.field_t.field_b.field, bf16[45,128,256]{2,1,0:T(8,128)(2,1)S(1)} %branch_1_fun.8.field_t.field_b.field, s32[128,256]{1,0:T(8,128)S(1)} %copy-done.3, ...), custom_call_target="tpu_custom_call" | custom-call | flops 1 | bytes 1048576 | tf_op jit(solution)/shard_map/cond/branch_1_fun/pallas_call | solution.py:469
  12.1 2.7 %collective-permute-start.6 = (bf16[23,8,256]{2,1,0:T(8,128)(2,1)S(1)}, bf16[23,8,256]{2,1,0:T(8,128)(2,1)S(1)}, u32[]{:S(2)}, u32[]{:S(2)}) collective-permute-start(bf16[23,8,256]{2,1,0:T(8,128)(2,1)S(1)} %get-tuple-element.62), channel_id=1, source_target_pairs={{0,16},{16,0},{32,48},{48,32},{64,80},{80,64},{96,112},{112,96},{1... | collective-permute-start | bytes 282632 | tf_op jit(solution)/shard_map/cond/branch_1_fun/ppermute | solution.py:27
  14.8 1.9 %collective-permute-start.7 = (bf16[23,8,256]{2,1,0:T(8,128)(2,1)S(1)}, bf16[23,8,256]{2,1,0:T(8,128)(2,1)S(1)}, u32[]{:S(2)}, u32[]{:S(2)}) collective-permute-start(bf16[23,8,256]{2,1,0:T(8,128)(2,1)S(1)} %get-tuple-element.63), channel_id=1, source_target_pairs={{16,32},{32,16},{48,64},{64,48},{80,96},{96,80},{17,33},{33,17},{4... | collective-permute-start | bytes 282632 | tf_op jit(solution)/shard_map/cond/branch_1_fun/ppermute | solution.py:27
  16.7 2.7 %branch_1_fun.10 = (bf16[1,128,256]{2,1,0:T(8,128)(2,1)S(1)}, bf16[9,128,128]{2,1,0:T(8,128)(2,1)S(1)}, bf16[3,128,128]{2,1,0:T(8,128)(2,1)S(1)}) custom-call(s32[8]{0:T(128)S(1)} %stack.92.info, bf16[45,128,256]{2,1,0:T(8,128)(2,1)S(1)} %branch_1_fun.8.field_t.field_b.field, s32[128,256]{1,0:T(8,128)S(1)} %copy-done.3, ...), custom_call_target="tpu_custom_call" | custom-call | flops 17179869184 | bytes 1048576 | tf_op jit(solution)/shard_map/cond/branch_1_fun/pallas_call | solution.py:488
  19.4 0.0 collective-permute-done.6.even
  19.4 3.1 %collective-permute-done.7.odd = bf16[23,8,256]{2,1,0:T(8,128)(2,1)S(1)} collective-permute-done((bf16[23,8,256]{2,1,0:T(8,128)(2,1)S(1)}, bf16[23,8,256]{2,1,0:T(8,128)(2,1)S(1)}, u32[]{:S(2)}, u32[]{:S(2)}) %collective-permute-start.7) | collective-permute-done | bytes 94240 | tf_op jit(solution)/shard_map/cond/branch_1_fun/ppermute | solution.py:27
  22.5 0.8 %branch_1_fun.11 = (bf16[45,8,256]{2,1,0:T(8,128)(2,1)S(1)}, bf16[9,8,128]{2,1,0:T(8,128)(2,1)S(1)}, bf16[3,136,128]{2,1,0:T(8,128)(2,1)S(1)}) custom-call(s32[8]{0:T(128)S(1)} %stack.92.info, bf16[23,8,256]{2,1,0:T(8,128)(2,1)S(1)} %collective-permute-done.6.even, bf16[23,8,256]{2,1,0:T(8,128)(2,1)S(1)} %collective-permute-done.7.odd, ...), custom_call_target="tpu_custom_call" | custom-call | flops 1 | bytes 1048576 | tf_op jit(solution)/shard_map/cond/branch_1_fun/pallas_call | solution.py:511
  23.3 3.2 %collective-permute-start.8 = (bf16[3,136,128]{2,1,0:T(8,128)(2,1)S(1)}, bf16[3,136,128]{2,1,0:T(8,128)(2,1)S(1)}, u32[]{:S(2)}, u32[]{:S(2)}) collective-permute-start(bf16[3,136,128]{2,1,0:T(8,128)(2,1)S(1)} %get-tuple-element.65), channel_id=1, source_target_pairs={{0,2},{2,0},{4,6},{6,4},{8,10},{10,8},{12,14},{14,12},{1,3},{3,1},... | collective-permute-start | bytes 313352 | tf_op jit(solution)/shard_map/cond/branch_1_fun/ppermute | solution.py:27
  26.5 3.0 %collective-permute-start.9 = (bf16[3,136,128]{2,1,0:T(8,128)(2,1)S(1)}, bf16[3,136,128]{2,1,0:T(8,128)(2,1)S(1)}, u32[]{:S(2)}, u32[]{:S(2)}) collective-permute-start(bf16[3,136,128]{2,1,0:T(8,128)(2,1)S(1)} %get-tuple-element.65), channel_id=1, source_target_pairs={{2,4},{4,2},{6,8},{8,6},{10,12},{12,10},{3,5},{5,3},{7,9},{9,7},{1... | collective-permute-start | bytes 313352 | tf_op jit(solution)/shard_map/cond/branch_1_fun/ppermute | solution.py:27
  29.6 9.4 %branch_1_fun.12.main = bf16[45,128,256]{2,1,0:T(8,128)(2,1)S(1)} custom-call(s32[8]{0:T(128)S(1)} %stack.92.info, f32[45]{0:T(128)S(1)} %copy-done.5, bf16[45,128,256]{2,1,0:T(8,128)(2,1)S(1)} %branch_1_fun.8.field_t.field_b.field, bf16[1,128,256]{2,1,0:T(8,128)(2,1)S(1)} %get-tuple-element.68.fixed, bf16[45,8,256]{2,1,0:T(8,128)(2,1)S(1)} %get-tuple-element.69.halo), custom_call_target="tpu_custom_call" | custom-call | flops 17179869184 | bytes 1048576 | tf_op jit(solution)/shard_map/cond/branch_1_fun/pallas_call | solution.py:526
  39.0 0.0 collective-permute-done.8.even
  39.0 0.0 collective-permute-done.9.odd
  39.0 4.9 %branch_1_fun.13 = bf16[45,128,256]{2,1,0:T(8,128)(2,1)} custom-call(s32[8]{0:T(128)S(1)} %stack.92.info, f32[2,9,8,128]{3,2,1,0:T(8,128)S(1)} %broadcast_in_dim.31.coefs, bf16[3,136,128]{2,1,0:T(8,128)(2,1)S(1)} %collective-permute-done.8.even, bf16[3,136,128]{2,1,0:T(8,128)(2,1)S(1)} %collective-permute-done.9.odd, ...), custom_call_target="tpu_custom_call" | custom-call | flops 1 | bytes 1048576 | tf_op jit(solution)/shard_map/cond/branch_1_fun/pallas_call | solution.py:565
  (4 shorter events, 0.0 us)
Async XLA Ops:
  2.1 7.1 %copy-start.5 = (f32[45]{0:T(128)S(1)}, f32[45]{0:T(128)}, u32[]{:S(2)}) copy-start(f32[45]{0:T(128)} %get-tuple-element.53.coefs) | copy-start | bytes 544 | tf_op jit(solution)/shard_map/cond
  2.1 7.4 %copy-start.3 = (s32[128,256]{1,0:T(8,128)S(1)}, s32[128,256]{1,0:T(8,128)}, u32[]{:S(2)}) copy-start(s32[128,256]{1,0:T(8,128)} %get-tuple-element.60.mask.mask_t.mask_b) | copy-start | bytes 393220 | tf_op jit(solution)/shard_map/cond
  7.8 3.6 %collective-permute-start.5 = (bf16[1,128,256]{2,1,0:T(8,128)(2,1)S(1)}, bf16[1,128,256]{2,1,0:T(8,128)(2,1)S(1)}, u32[]{:S(2)}, u32[]{:S(2)}) collective-permute-start(bf16[1,128,256]{2,1,0:T(8,128)(2,1)S(1)} %get-tuple-element.61), channel_id=1, source_target_pairs={{0,1},{1,0},{2,3},{3,2},{4,5},{5,4},{6,7},{7,6},{8,9},{9,8},{10,11... | collective-permute-start | bytes 196616 | tf_op jit(solution)/shard_map/cond/branch_1_fun/ppermute | solution.py:27
  12.1 7.3 %collective-permute-start.6 = (bf16[23,8,256]{2,1,0:T(8,128)(2,1)S(1)}, bf16[23,8,256]{2,1,0:T(8,128)(2,1)S(1)}, u32[]{:S(2)}, u32[]{:S(2)}) collective-permute-start(bf16[23,8,256]{2,1,0:T(8,128)(2,1)S(1)} %get-tuple-element.62), channel_id=1, source_target_pairs={{0,16},{16,0},{32,48},{48,32},{64,80},{80,64},{96,112},{112,96},{1... | collective-permute-start | bytes 282632 | tf_op jit(solution)/shard_map/cond/branch_1_fun/ppermute | solution.py:27
  14.8 7.7 %collective-permute-start.7 = (bf16[23,8,256]{2,1,0:T(8,128)(2,1)S(1)}, bf16[23,8,256]{2,1,0:T(8,128)(2,1)S(1)}, u32[]{:S(2)}, u32[]{:S(2)}) collective-permute-start(bf16[23,8,256]{2,1,0:T(8,128)(2,1)S(1)} %get-tuple-element.63), channel_id=1, source_target_pairs={{16,32},{32,16},{48,64},{64,48},{80,96},{96,80},{17,33},{33,17},{4... | collective-permute-start | bytes 282632 | tf_op jit(solution)/shard_map/cond/branch_1_fun/ppermute | solution.py:27
  23.3 15.6 %collective-permute-start.8 = (bf16[3,136,128]{2,1,0:T(8,128)(2,1)S(1)}, bf16[3,136,128]{2,1,0:T(8,128)(2,1)S(1)}, u32[]{:S(2)}, u32[]{:S(2)}) collective-permute-start(bf16[3,136,128]{2,1,0:T(8,128)(2,1)S(1)} %get-tuple-element.65), channel_id=1, source_target_pairs={{0,2},{2,0},{4,6},{6,4},{8,10},{10,8},{12,14},{14,12},{1,3},{3,1},... | collective-permute-start | bytes 313352 | tf_op jit(solution)/shard_map/cond/branch_1_fun/ppermute | solution.py:27
  26.5 12.5 %collective-permute-start.9 = (bf16[3,136,128]{2,1,0:T(8,128)(2,1)S(1)}, bf16[3,136,128]{2,1,0:T(8,128)(2,1)S(1)}, u32[]{:S(2)}, u32[]{:S(2)}) collective-permute-start(bf16[3,136,128]{2,1,0:T(8,128)(2,1)S(1)} %get-tuple-element.65), channel_id=1, source_target_pairs={{2,4},{4,2},{6,8},{8,6},{10,12},{12,10},{3,5},{5,3},{7,9},{9,7},{1... | collective-permute-start | bytes 313352 | tf_op jit(solution)/shard_map/cond/branch_1_fun/ppermute | solution.py:27

commit v3 on v2

--- a/solution.py
+++ b/solution.py
@@ -69,17 +69,23 @@
 
 
 def remap_kernel(
-    count, total, info, begins, levels, inside, thick, child, own, part, acc, low, high
+    count, total, info, begins, levels, inside, thick, child, own, part, acc, low, high, held, sems
 ):
     children, parents = child.shape[0], own.shape[0]
     size, width = low.shape
 
-    @pl.when(pl.program_id(0) == 0)
-    def _():
-        below, above = share_columns((levels, inside, thick), size, total)
-        low[...] = jnp.broadcast_to(below, low.shape)
-        high[...] = jnp.broadcast_to(above, high.shape)
-
+    block = acc.shape[1]
+    chunks = held.shape[1] // block
+
+    def copy(i):
+        rows = pl.ds(pl.multiple_of(i * block, block), block)
+        return pltpu.make_async_copy(child.at[:, rows, :], held.at[:, rows, :], sems.at[i])
+
+    for i in range(chunks):
+        copy(i).start()
+    below, above = share_columns((levels, inside, thick), size, total)
+    low[...] = jnp.broadcast_to(below, low.shape)
+    high[...] = jnp.broadcast_to(above, high.shape)
     slab = info[7]
     origin = slab * children
     trash = parents + count
@@ -95,33 +101,40 @@
     end = parents + jnp.where(slab == 0, count, jnp.clip(first + count, 0, count))
     lax.fori_loop(untouched, end, clear, 0)
 
-    def step(k, state):
-        here, above = state
-        level = begins[origin + k]
-        rose = level != begins[jnp.maximum(origin + k - 1, 0)]
-        value = child[k].astype(F32)
-        here = jnp.where(rose, above, here) + low[pl.ds(origin + k, 1), :] * value
-        above = jnp.where(rose, 0.0, above) + high[pl.ds(origin + k, 1), :] * value
-        place = level - slab * parents
-        place = jnp.where(place >= 0, place, parents + count + place)
-        acc[jnp.clip(place, 0, trash)] = here
-        return here, above
-
-    zero = jnp.zeros(acc.shape[1:], F32)
-    here, above = lax.fori_loop(0, children, step, (zero, zero), unroll=4)
-    acc[jnp.where(slab == 0, jnp.clip(last + 1, 0, trash), trash)] = above
-
-    def keep(p, carry):
-        own[p] = acc[p].astype(BF16)
-        return carry
-
-    lax.fori_loop(0, parents, keep, 0, unroll=5)
-
-    def pass_on(j, carry):
-        part[j] = acc[parents + j].astype(BF16)
-        return carry
-
-    lax.fori_loop(0, count, pass_on, 0)
+    def chunk(i, carry):
+        copy(i).wait()
+        rows = pl.ds(pl.multiple_of(i * block, block), block)
+
+        def step(k, state):
+            here, above = state
+            level = begins[origin + k]
+            rose = level != begins[jnp.maximum(origin + k - 1, 0)]
+            value = held[k, rows, :].astype(F32)
+            here = jnp.where(rose, above, here) + low[pl.ds(origin + k, 1), :] * value
+            above = jnp.where(rose, 0.0, above) + high[pl.ds(origin + k, 1), :] * value
+            place = level - slab * parents
+            place = jnp.where(place >= 0, place, parents + count + place)
+            acc[jnp.clip(place, 0, trash)] = here
+            return here, above
+
+        zero = jnp.zeros(acc.shape[1:], F32)
+        here, above = lax.fori_loop(0, children, step, (zero, zero), unroll=4)
+        acc[jnp.where(slab == 0, jnp.clip(last + 1, 0, trash), trash)] = above
+
+        def keep(p, carry):
+            own[p, rows, :] = acc[p].astype(BF16)
+            return carry
+
+        lax.fori_loop(0, parents, keep, 0, unroll=5)
+
+        def pass_on(j, carry):
+            part[j, rows, :] = acc[parents + j].astype(BF16)
+            return carry
+
+        lax.fori_loop(0, count, pass_on, 0)
+        return carry
+
+    lax.fori_loop(0, chunks, chunk, 0)
 
 
 def blend_kernel(group, own, par, mask, field, old, sems):
@@ -277,127 +290,125 @@
 
 
 def smooth_kernel(count, info, coefs, field, fixed, halo, out, left, right, work, sides, near):
-    levels, rows = field.shape[:2]
+    levels, rows = left.shape[0], field.shape[1]
     deals = left.shape[1] // SUB
     flags = row_flags(info, deals, rows)
     flags = [None if f is None else jnp.concatenate([f, f], axis=1) for f in flags]
-    base = pl.program_id(0) * levels
-
-    @pl.when(pl.program_id(0) == 0)
-    def _():
-        r = lax.broadcasted_iota(jnp.int32, near.shape, 0)
-        c = lax.broadcasted_iota(jnp.int32, near.shape, 1)
-        near[...] = jnp.where(jnp.abs(r - c) == 1, 1.0, 0.0).astype(BF16)
-
-    weights = []
-    for p in range(levels):
-        scale = coefs[base + p]
-        keep = 1.0 - 4.0 * scale
-        weights.append(
-            (
-                [scale if f is None else scale * f for f in flags],
-                [keep if f is None else keep * f for f in flags],
+    r = lax.broadcasted_iota(jnp.int32, near.shape, 0)
+    c = lax.broadcasted_iota(jnp.int32, near.shape, 1)
+    near[...] = jnp.where(jnp.abs(r - c) == 1, 1.0, 0.0).astype(BF16)
+
+    def group(g, carry):
+        base = g * levels
+        weights = []
+        for p in range(levels):
+            scale = coefs[base + p]
+            keep = 1.0 - 4.0 * scale
+            weights.append(
+                (
+                    [scale if f is None else scale * f for f in flags],
+                    [keep if f is None else keep * f for f in flags],
+                )
             )
-        )
-        j = base + p - info[2]
-        use_fixed = (j >= 0) & (j < count)
-        j = jnp.clip(j, 0, count - 1)
-        for ref, cut in ((left, slice(0, LANES)), (right, slice(LANES, 2 * LANES))):
-            ref[p, :rows, :] = field[p, :, cut].astype(F32)
-
-            @pl.when(use_fixed)
-            def _():
-                ref[p, :rows, :] = fixed[j, :, cut].astype(F32)
-
-            ref[p, rows:, :] = halo[p, :, cut].astype(F32)
-        for i in range(deals):
-            part = slice(SUB * i, SUB * i + SUB)
-            work[0, p, part, :LANES] = left[p, pl.ds(i, SUB, stride=deals), :]
-            work[0, p, part, LANES:] = right[p, pl.ds(i, SUB, stride=deals), :]
-    for s in range(SMOOTH):
-        flat = work[s % 2].reshape(levels * deals * SUB, 2 * LANES).astype(BF16)
-        side = jnp.dot(flat, near[...], preferred_element_type=F32)
-        sides[...] = side.reshape(sides.shape)
+            j = base + p - info[2]
+            use_fixed = (j >= 0) & (j < count)
+            j = jnp.clip(j, 0, count - 1)
+            for ref, cut in ((left, slice(0, LANES)), (right, slice(LANES, 2 * LANES))):
+                ref[p, :rows, :] = field[base + p, :, cut].astype(F32)
+
+                @pl.when(use_fixed)
+                def _():
+                    ref[p, :rows, :] = fixed[j, :, cut].astype(F32)
+
+                ref[p, rows:, :] = halo[base + p, :, cut].astype(F32)
+            for i in range(deals):
+                part = slice(SUB * i, SUB * i + SUB)
+                work[0, p, part, :LANES] = left[p, pl.ds(i, SUB, stride=deals), :]
+                work[0, p, part, LANES:] = right[p, pl.ds(i, SUB, stride=deals), :]
+        for s in range(SMOOTH):
+            flat = work[s % 2].reshape(levels * deals * SUB, 2 * LANES).astype(BF16)
+            side = jnp.dot(flat, near[...], preferred_element_type=F32)
+            sides[...] = side.reshape(sides.shape)
+            for p in range(levels):
+                values = [work[s % 2, p, SUB * i : SUB * i + SUB, :] for i in range(deals)]
+                values = row_sweep(
+                    values, lambda i, _: sides[p, SUB * i : SUB * i + SUB, :], *weights[p]
+                )
+                for i, value in enumerate(values):
+                    if s == SMOOTH - 1:
+                        left[p, pl.ds(i, SUB, stride=deals), :] = value[:, :LANES]
+                        right[p, pl.ds(i, SUB, stride=deals), :] = value[:, LANES:]
+                    else:
+                        work[(s + 1) % 2, p, SUB * i : SUB * i + SUB, :] = value
         for p in range(levels):
-            values = [work[s % 2, p, SUB * i : SUB * i + SUB, :] for i in range(deals)]
-            values = row_sweep(
-                values, lambda i, _: sides[p, SUB * i : SUB * i + SUB, :], *weights[p]
-            )
-            for i, value in enumerate(values):
-                if s == SMOOTH - 1:
-                    left[p, pl.ds(i, SUB, stride=deals), :] = value[:, :LANES]
-                    right[p, pl.ds(i, SUB, stride=deals), :] = value[:, LANES:]
-                else:
-                    work[(s + 1) % 2, p, SUB * i : SUB * i + SUB, :] = value
-    for p in range(levels):
-        out[p, :, :LANES] = left[p, :rows, :].astype(BF16)
-        out[p, :, LANES:] = right[p, :rows, :].astype(BF16)
+            out[base + p, :, :LANES] = left[p, :rows, :].astype(BF16)
+            out[base + p, :, LANES:] = right[p, :rows, :].astype(BF16)
+        return carry
+
+    lax.fori_loop(0, field.shape[0] // levels, group, 0)
 
 
 def seam_kernel(info, coefs, even, odd, core, edge, main, out, tiles, work, done, sems):
     total = tiles.shape[0]
     rows = core.shape[1]
     count = tiles.shape[1] // SUB
-    step = pl.program_id(0)
-
-    @pl.when(step == 0)
-    def _():
-        flip = info[1] == 1
-        flags = row_flags(info, count, rows)
-        slot = lax.broadcasted_iota(jnp.int32, tiles.shape[1:], 1) % SLOT
-        for q in range(even.shape[0]):
-            a, b = even[q].astype(F32), odd[q].astype(F32)
-            after, before = jnp.where(flip, b, a), jnp.where(flip, a, b)
-            for u in range(min(PER_SENT, total - q * PER_SENT)):
-                t = q * PER_SENT + u
-                own = jnp.concatenate([core[t].astype(F32), edge[t].astype(F32)], axis=0)
-                right = pltpu.roll(after, (4 - 8 * u) % LANES, 1)
-                left = pltpu.roll(before, (12 - 8 * u) % LANES, 1)
-                tile = jnp.where(slot < 12, right, left)
-                tiles[t] = jnp.where((slot >= 8) & (slot < 16), tile, own)
+    flip = info[1] == 1
+    flags = row_flags(info, count, rows)
+    slot = lax.broadcasted_iota(jnp.int32, tiles.shape[1:], 1) % SLOT
+    for q in range(even.shape[0]):
+        a, b = even[q].astype(F32), odd[q].astype(F32)
+        after, before = jnp.where(flip, b, a), jnp.where(flip, a, b)
+        for u in range(min(PER_SENT, total - q * PER_SENT)):
+            t = q * PER_SENT + u
+            own = jnp.concatenate([core[t].astype(F32), edge[t].astype(F32)], axis=0)
+            right = pltpu.roll(after, (4 - 8 * u) % LANES, 1)
+            left = pltpu.roll(before, (12 - 8 * u) % LANES, 1)
+            tile = jnp.where(slot < 12, right, left)
+            tiles[t] = jnp.where((slot >= 8) & (slot < 16), tile, own)
+    for t in range(total):
+        for i in range(count):
+            work[0, t, i] = tiles[t, pl.ds(i, SUB, stride=count), :]
+    for s in range(SMOOTH):
         for t in range(total):
+            scale = coefs[0, t]
+            keep = coefs[1, t]
+            scales = [scale if f is None else scale * f for f in flags]
+            keeps = [keep if f is None else keep * f for f in flags]
+            values = [work[s % 2, t, i] for i in range(count)]
+            new = row_sweep(
+                values,
+                lambda _, x: pltpu.roll(x, 1, 1) + pltpu.roll(x, LANES - 1, 1),
+                scales,
+                keeps,
+            )
             for i in range(count):
-                work[0, t, i] = tiles[t, pl.ds(i, SUB, stride=count), :]
-        for s in range(SMOOTH):
-            for t in range(total):
-                scale = coefs[0, t]
-                keep = coefs[1, t]
-                scales = [scale if f is None else scale * f for f in flags]
-                keeps = [keep if f is None else keep * f for f in flags]
-                values = [work[s % 2, t, i] for i in range(count)]
-                new = row_sweep(
-                    values,
-                    lambda _, x: pltpu.roll(x, 1, 1) + pltpu.roll(x, LANES - 1, 1),
-                    scales,
-                    keeps,
-                )
-                for i in range(count):
-                    if s < SMOOTH - 1:
-                        work[(s + 1) % 2, t, i] = new[i]
-                    else:
-                        tiles[t, pl.ds(i, SUB, stride=count), :] = new[i]
-
-    seam = tiles[step, :rows, :]
-    lane = lax.broadcasted_iota(jnp.int32, seam.shape, 1)
-    seam = jnp.where(lane % SLOT < 8, seam, pltpu.roll(seam, LANES - 8, 1))
-    group = main.shape[0]
-    for j in range(group):
-        both = pltpu.roll(seam, (120 - SLOT * j) % LANES, 1)
-        a, b = main[j, :, :LANES].astype(F32), main[j, :, LANES:].astype(F32)
-        p = step * group + j
-        done[p, :, :LANES] = jnp.where(lane < SMOOTH, both, a).astype(BF16)
-        done[p, :, LANES:] = jnp.where(lane >= LANES - SMOOTH, both, b).astype(BF16)
+                if s < SMOOTH - 1:
+                    work[(s + 1) % 2, t, i] = new[i]
+                else:
+                    tiles[t, pl.ds(i, SUB, stride=count), :] = new[i]
+
+    group = main.shape[0] // total
 
     def copy(i):
         levels = pl.ds(i * group, group)
         return pltpu.make_async_copy(done.at[levels], out.at[levels], sems.at[i])
 
-    copy(step).start()
-
-    @pl.when(step == total - 1)
-    def _():
-        for i in range(total):
-            copy(i).wait()
+    def step(i, carry):
+        seam = tiles[i, :rows, :]
+        lane = lax.broadcasted_iota(jnp.int32, seam.shape, 1)
+        seam = jnp.where(lane % SLOT < 8, seam, pltpu.roll(seam, LANES - 8, 1))
+        for j in range(group):
+            both = pltpu.roll(seam, (120 - SLOT * j) % LANES, 1)
+            p = i * group + j
+            a, b = main[p, :, :LANES].astype(F32), main[p, :, LANES:].astype(F32)
+            done[p, :, :LANES] = jnp.where(lane < SMOOTH, both, a).astype(BF16)
+            done[p, :, LANES:] = jnp.where(lane >= LANES - SMOOTH, both, b).astype(BF16)
+        copy(i).start()
+        return carry
+
+    lax.fori_loop(0, total, step, 0)
+    for i in range(total):
+        copy(i).wait()
 
 
 def device_facts(start):
@@ -425,21 +436,23 @@
     block = ROW_BLOCK
     own, part = call(
         functools.partial(remap_kernel, count, total),
-        (rows // block,),
+        (1,),
         [
             smem(), smem(), whole(size), whole(size), whole(size),
-            pl.BlockSpec((children, block, columns), lambda i: (0, i, 0)),
-        ],
-        [
-            pl.BlockSpec((parents, block, columns), lambda i: (0, i, 0)),
-            pl.BlockSpec((count, block, columns), lambda i: (0, i, 0)),
-        ],
+            pl.BlockSpec(memory_space=pltpu.HBM),
+        ],
+        [whole(parents, rows, columns), whole(count, rows, columns)],
         [
             jax.ShapeDtypeStruct((parents, rows, columns), BF16),
             jax.ShapeDtypeStruct((count, rows, columns), BF16),
         ],
-        [pltpu.VMEM((parents + count + 1, block, columns), F32)]
-        + [pltpu.VMEM((size, columns), F32)] * 2,
+        [
+            pltpu.VMEM((parents + count + 1, block, columns), F32),
+            pltpu.VMEM((size, columns), F32),
+            pltpu.VMEM((size, columns), F32),
+            pltpu.VMEM((children, rows, columns), BF16),
+            pltpu.SemaphoreType.DMA((rows // block,)),
+        ],
     )(info, level_map, level_map, inside, thick, child)
     part = pair_swap(part, "lev", 0)
     group = PER_TILE
@@ -525,14 +538,14 @@
     group = PER_TILE
     main = call(
         functools.partial(smooth_kernel, count),
-        (parents // group,),
+        (1,),
         [
             smem(), smem(),
-            pl.BlockSpec((group, rows, columns), lambda i: (i, 0, 0)),
+            whole(parents, rows, columns),
             whole(count, rows, columns),
-            pl.BlockSpec((group, SUB, columns), lambda i: (i, 0, 0)),
-        ],
-        pl.BlockSpec((group, rows, columns), lambda i: (i, 0, 0)),
+            whole(parents, SUB, columns),
+        ],
+        whole(parents, rows, columns),
         jax.ShapeDtypeStruct((parents, rows, columns), BF16),
         [pltpu.VMEM((group, extended, LANES), F32)] * 2
         + [
@@ -564,7 +577,7 @@
     lane_coefs = jnp.broadcast_to(lane_coefs[:, :, None, :], (2, seams, SUB, LANES))
     return call(
         seam_kernel,
-        (seams,),
+        (1,),
         [
             smem(),
             whole(2, seams, SUB, LANES),
@@ -572,7 +585,7 @@
             whole(sents, extended, LANES),
             whole(seams, rows, LANES),
             whole(seams, SUB, LANES),
-            pl.BlockSpec((group, rows, columns), lambda i: (i, 0, 0)),
+            whole(parents, rows, columns),
         ],
         pl.BlockSpec(memory_space=pltpu.HBM),
         pltpu.HBM((parents, rows, columns), BF16),

time: 44.2 us -> 43.4 us (0.982)
  Pallas kernels: 26 us -> 25.3 us
    pallas_call x3, Pallas kernels: 19.9 us -> 19.2 us  [the longest x1 9.16 us: feed_back(): call(functools.partial(smooth_kernel, count), (1,), [smem(), smem(), whol...]
where the time goes in v3:
time: 43.4 us; the launch traced here: 43.2 us
  Pallas kernels  25.3 us (58%)
  starting transfers between devices  12.2 us (28%)
  waiting for transfers between devices  3.12 us (7%)
  other arithmetic  1.45 us (3%)
  between operations  0.65 us (1%)
    ppermute x5, starting transfers between devices, pair_swap(): return lax.ppermute(x, axis, route)  12.2 us
    pallas_call x1, Pallas kernels, feed_back(): call(functools.partial(smooth_kernel, count), (1,), [smem(), smem(), whol...  9.16 us
    pallas_call x1, Pallas kernels, feed_back(): call(functools.partial(remap_kernel, count, total), (1,), [smem(), smem()...  5.32 us
    pallas_call x1, Pallas kernels, finish(): call(seam_kernel, (1,), [smem(), whole(2, seams, SUB, LANES), whole(sents...  4.69 us
    ppermute x5, waiting for transfers between devices, pair_swap(): return lax.ppermute(x, axis, route)  3.12 us
    pallas_call x1, Pallas kernels, feed_back(): call(functools.partial(edge_kernel, count), (rows // block,), [smem(), pl...  2.67 us
    pallas_call x1, Pallas kernels, feed_back(): call(functools.partial(blend_kernel, group), (1,), [whole(parents, rows,...  1.94 us
    reduce_max x1, other arithmetic, shards(): jnp.max(ends * jnp.array([1, -1]) + jnp.array([2 - parents, parents]))  1.42 us
  transfers between devices with their start and end apart: 5, of which 1 were waited for; matrix products, arithmetic and copies ran while one was open for 1% of the time, Pallas kernels for 32%

profile of v3, /device:TPU:35, one launch (start us, length us, event | category | flops | bytes accessed | tf_op | source)
XLA Modules:
  0.0 43.2 jit_solution(15579104822133055185)
XLA Ops:
  0.0 1.4 %add_reduce_fusion = s32[]{:T(128)} fusion(s32[2]{0:T(128)} %constant.124.clone, s32[2]{0:T(128)} %constant.123.clone, s32[136]{0:T(256)} %param.13), kind=kLoop, calls=%fused_computation.10 | loop fusion | flops 5 | bytes 28 | tf_op jit(solution)/shard_map/reduce_max | solution.py:605
  2.1 41.1 %conditional.1 = (bf16[45,128,256]{2,1,0:T(8,128)(2,1)}) conditional(s32[]{:T(128)} %convert_element_type.4, (f32[45]{0:T(128)}, s32[136]{0:T(256)}, f32[136]{0:T(256)}, f32[136]{0:T(256)}, bf16[68,128,256]{2,1,0:T(8,128)(2,1)}, /*index=5*/bf16[45,128,256]{2,1,0:T(8,128)(2,1)}, s32[128,256]{1,0:T(8,128)}) %tuple.11, (f32[45]{0:T(128)}, s32[136]{0:T(256)}, ...), branch_computations={%region_1.2_spmd, %region_2.3_spmd} | conditional | flops 51539615744 | bytes 39468136 | solution.py:612
  2.1 0.0 copy-start.5
  2.1 0.0 copy-start.3
  2.1 0.1 stack.92.info
  2.2 5.3 %branch_1_fun.7 = (bf16[45,128,256]{2,1,0:T(8,128)(2,1)S(1)}, bf16[1,128,256]{2,1,0:T(8,128)(2,1)S(1)}) custom-call(s32[8]{0:T(128)S(1)} %stack.92.info, s32[136]{0:T(256)} %get-tuple-element.54.begins.levels, s32[136]{0:T(256)} %get-tuple-element.54.begins.levels, f32[136]{0:T(256)} %get-tuple-element.55.inside, f32[136]{0:T(256)} %get-tuple-element.56.thick, ...), custom_call_target="tpu_custom_call" | custom-call | flops 1 | bytes 1048576 | tf_op jit(solution)/shard_map/cond/branch_1_fun/pallas_call | solution.py:437
  7.6 1.4 %collective-permute-start.5 = (bf16[1,128,256]{2,1,0:T(8,128)(2,1)S(1)}, bf16[1,128,256]{2,1,0:T(8,128)(2,1)S(1)}, u32[]{:S(2)}, u32[]{:S(2)}) collective-permute-start(bf16[1,128,256]{2,1,0:T(8,128)(2,1)S(1)} %get-tuple-element.61), channel_id=1, source_target_pairs={{0,1},{1,0},{2,3},{3,2},{4,5},{5,4},{6,7},{7,6},{8,9},{9,8},{10,11... | collective-permute-start | bytes 196616 | tf_op jit(solution)/shard_map/cond/branch_1_fun/ppermute | solution.py:27
  9.0 0.0 copy-done.5
  9.0 0.1 reshape.44
  9.0 0.1 broadcast_in_dim.29
  9.1 0.1 reshape.45
  9.2 0.0 copy-done.3
  9.2 1.9 %branch_1_fun.8.field_t.field_b.field = bf16[45,128,256]{2,1,0:T(8,128)(2,1)S(1)} custom-call(bf16[45,128,256]{2,1,0:T(8,128)(2,1)S(1)} %get-tuple-element.58.own, bf16[45,128,256]{2,1,0:T(8,128)(2,1)} %get-tuple-element.59.par, s32[128,256]{1,0:T(8,128)S(1)} %copy-done.3), custom_call_target="tpu_custom_call" | custom-call | flops 17179869184 | bytes 1048576 | tf_op jit(solution)/shard_map/cond/branch_1_fun/pallas_call | solution.py:459
  11.2 0.0 collective-permute-done.5.part_t.part_b.part
  11.2 0.7 %branch_1_fun.9 = (bf16[23,8,256]{2,1,0:T(8,128)(2,1)S(1)}, bf16[23,8,256]{2,1,0:T(8,128)(2,1)S(1)}) custom-call(s32[8]{0:T(128)S(1)} %stack.92.info, bf16[45,128,256]{2,1,0:T(8,128)(2,1)S(1)} %branch_1_fun.8.field_t.field_b.field, bf16[45,128,256]{2,1,0:T(8,128)(2,1)S(1)} %branch_1_fun.8.field_t.field_b.field, s32[128,256]{1,0:T(8,128)S(1)} %copy-done.3, ...), custom_call_target="tpu_custom_call" | custom-call | flops 1 | bytes 1048576 | tf_op jit(solution)/shard_map/cond/branch_1_fun/pallas_call | solution.py:482
  11.9 2.7 %collective-permute-start.6 = (bf16[23,8,256]{2,1,0:T(8,128)(2,1)S(1)}, bf16[23,8,256]{2,1,0:T(8,128)(2,1)S(1)}, u32[]{:S(2)}, u32[]{:S(2)}) collective-permute-start(bf16[23,8,256]{2,1,0:T(8,128)(2,1)S(1)} %get-tuple-element.62), channel_id=1, source_target_pairs={{0,16},{16,0},{32,48},{48,32},{64,80},{80,64},{96,112},{112,96},{1... | collective-permute-start | bytes 282632 | tf_op jit(solution)/shard_map/cond/branch_1_fun/ppermute | solution.py:27
  14.6 1.9 %collective-permute-start.7 = (bf16[23,8,256]{2,1,0:T(8,128)(2,1)S(1)}, bf16[23,8,256]{2,1,0:T(8,128)(2,1)S(1)}, u32[]{:S(2)}, u32[]{:S(2)}) collective-permute-start(bf16[23,8,256]{2,1,0:T(8,128)(2,1)S(1)} %get-tuple-element.63), channel_id=1, source_target_pairs={{16,32},{32,16},{48,64},{64,48},{80,96},{96,80},{17,33},{33,17},{4... | collective-permute-start | bytes 282632 | tf_op jit(solution)/shard_map/cond/branch_1_fun/ppermute | solution.py:27
  16.5 2.7 %branch_1_fun.10 = (bf16[1,128,256]{2,1,0:T(8,128)(2,1)S(1)}, bf16[9,128,128]{2,1,0:T(8,128)(2,1)S(1)}, bf16[3,128,128]{2,1,0:T(8,128)(2,1)S(1)}) custom-call(s32[8]{0:T(128)S(1)} %stack.92.info, bf16[45,128,256]{2,1,0:T(8,128)(2,1)S(1)} %branch_1_fun.8.field_t.field_b.field, s32[128,256]{1,0:T(8,128)S(1)} %copy-done.3, ...), custom_call_target="tpu_custom_call" | custom-call | flops 17179869184 | bytes 1048576 | tf_op jit(solution)/shard_map/cond/branch_1_fun/pallas_call | solution.py:501
  19.2 0.0 collective-permute-done.6.even
  19.2 3.1 %collective-permute-done.7.odd = bf16[23,8,256]{2,1,0:T(8,128)(2,1)S(1)} collective-permute-done((bf16[23,8,256]{2,1,0:T(8,128)(2,1)S(1)}, bf16[23,8,256]{2,1,0:T(8,128)(2,1)S(1)}, u32[]{:S(2)}, u32[]{:S(2)}) %collective-permute-start.7) | collective-permute-done | bytes 94240 | tf_op jit(solution)/shard_map/cond/branch_1_fun/ppermute | solution.py:27
  22.3 0.8 %branch_1_fun.11 = (bf16[45,8,256]{2,1,0:T(8,128)(2,1)S(1)}, bf16[9,8,128]{2,1,0:T(8,128)(2,1)S(1)}, bf16[3,136,128]{2,1,0:T(8,128)(2,1)S(1)}) custom-call(s32[8]{0:T(128)S(1)} %stack.92.info, bf16[23,8,256]{2,1,0:T(8,128)(2,1)S(1)} %collective-permute-done.6.even, bf16[23,8,256]{2,1,0:T(8,128)(2,1)S(1)} %collective-permute-done.7.odd, ...), custom_call_target="tpu_custom_call" | custom-call | flops 1 | bytes 1048576 | tf_op jit(solution)/shard_map/cond/branch_1_fun/pallas_call | solution.py:524
  23.1 3.2 %collective-permute-start.8 = (bf16[3,136,128]{2,1,0:T(8,128)(2,1)S(1)}, bf16[3,136,128]{2,1,0:T(8,128)(2,1)S(1)}, u32[]{:S(2)}, u32[]{:S(2)}) collective-permute-start(bf16[3,136,128]{2,1,0:T(8,128)(2,1)S(1)} %get-tuple-element.65), channel_id=1, source_target_pairs={{0,2},{2,0},{4,6},{6,4},{8,10},{10,8},{12,14},{14,12},{1,3},{3,1},... | collective-permute-start | bytes 313352 | tf_op jit(solution)/shard_map/cond/branch_1_fun/ppermute | solution.py:27
  26.3 3.0 %collective-permute-start.9 = (bf16[3,136,128]{2,1,0:T(8,128)(2,1)S(1)}, bf16[3,136,128]{2,1,0:T(8,128)(2,1)S(1)}, u32[]{:S(2)}, u32[]{:S(2)}) collective-permute-start(bf16[3,136,128]{2,1,0:T(8,128)(2,1)S(1)} %get-tuple-element.65), channel_id=1, source_target_pairs={{2,4},{4,2},{6,8},{8,6},{10,12},{12,10},{3,5},{5,3},{7,9},{9,7},{1... | collective-permute-start | bytes 313352 | tf_op jit(solution)/shard_map/cond/branch_1_fun/ppermute | solution.py:27
  29.3 9.2 %branch_1_fun.12.main = bf16[45,128,256]{2,1,0:T(8,128)(2,1)S(1)} custom-call(s32[8]{0:T(128)S(1)} %stack.92.info, f32[45]{0:T(128)S(1)} %copy-done.5, bf16[45,128,256]{2,1,0:T(8,128)(2,1)S(1)} %branch_1_fun.8.field_t.field_b.field, bf16[1,128,256]{2,1,0:T(8,128)(2,1)S(1)} %get-tuple-element.68.fixed, bf16[45,8,256]{2,1,0:T(8,128)(2,1)S(1)} %get-tuple-element.69.halo), custom_call_target="tpu_custom_call" | custom-call | flops 17179869184 | bytes 1048576 | tf_op jit(solution)/shard_map/cond/branch_1_fun/pallas_call | solution.py:539
  38.5 0.0 collective-permute-done.8.even
  38.5 0.0 collective-permute-done.9.odd
  38.5 4.7 %branch_1_fun.13 = bf16[45,128,256]{2,1,0:T(8,128)(2,1)} custom-call(s32[8]{0:T(128)S(1)} %stack.92.info, f32[2,9,8,128]{3,2,1,0:T(8,128)S(1)} %broadcast_in_dim.31.coefs, bf16[3,136,128]{2,1,0:T(8,128)(2,1)S(1)} %collective-permute-done.8.even, bf16[3,136,128]{2,1,0:T(8,128)(2,1)S(1)} %collective-permute-done.9.odd, ...), custom_call_target="tpu_custom_call" | custom-call | flops 1 | bytes 1048576 | tf_op jit(solution)/shard_map/cond/branch_1_fun/pallas_call | solution.py:578
  (4 shorter events, 0.0 us)
Async XLA Ops:
  2.1 6.9 %copy-start.5 = (f32[45]{0:T(128)S(1)}, f32[45]{0:T(128)}, u32[]{:S(2)}) copy-start(f32[45]{0:T(128)} %get-tuple-element.53.coefs) | copy-start | bytes 544 | tf_op jit(solution)/shard_map/cond
  2.1 7.1 %copy-start.3 = (s32[128,256]{1,0:T(8,128)S(1)}, s32[128,256]{1,0:T(8,128)}, u32[]{:S(2)}) copy-start(s32[128,256]{1,0:T(8,128)} %get-tuple-element.60.mask.mask_t.mask_b) | copy-start | bytes 393220 | tf_op jit(solution)/shard_map/cond
  7.6 3.6 %collective-permute-start.5 = (bf16[1,128,256]{2,1,0:T(8,128)(2,1)S(1)}, bf16[1,128,256]{2,1,0:T(8,128)(2,1)S(1)}, u32[]{:S(2)}, u32[]{:S(2)}) collective-permute-start(bf16[1,128,256]{2,1,0:T(8,128)(2,1)S(1)} %get-tuple-element.61), channel_id=1, source_target_pairs={{0,1},{1,0},{2,3},{3,2},{4,5},{5,4},{6,7},{7,6},{8,9},{9,8},{10,11... | collective-permute-start | bytes 196616 | tf_op jit(solution)/shard_map/cond/branch_1_fun/ppermute | solution.py:27
  11.9 7.3 %collective-permute-start.6 = (bf16[23,8,256]{2,1,0:T(8,128)(2,1)S(1)}, bf16[23,8,256]{2,1,0:T(8,128)(2,1)S(1)}, u32[]{:S(2)}, u32[]{:S(2)}) collective-permute-start(bf16[23,8,256]{2,1,0:T(8,128)(2,1)S(1)} %get-tuple-element.62), channel_id=1, source_target_pairs={{0,16},{16,0},{32,48},{48,32},{64,80},{80,64},{96,112},{112,96},{1... | collective-permute-start | bytes 282632 | tf_op jit(solution)/shard_map/cond/branch_1_fun/ppermute | solution.py:27
  14.6 7.7 %collective-permute-start.7 = (bf16[23,8,256]{2,1,0:T(8,128)(2,1)S(1)}, bf16[23,8,256]{2,1,0:T(8,128)(2,1)S(1)}, u32[]{:S(2)}, u32[]{:S(2)}) collective-permute-start(bf16[23,8,256]{2,1,0:T(8,128)(2,1)S(1)} %get-tuple-element.63), channel_id=1, source_target_pairs={{16,32},{32,16},{48,64},{64,48},{80,96},{96,80},{17,33},{33,17},{4... | collective-permute-start | bytes 282632 | tf_op jit(solution)/shard_map/cond/branch_1_fun/ppermute | solution.py:27
  23.1 15.4 %collective-permute-start.8 = (bf16[3,136,128]{2,1,0:T(8,128)(2,1)S(1)}, bf16[3,136,128]{2,1,0:T(8,128)(2,1)S(1)}, u32[]{:S(2)}, u32[]{:S(2)}) collective-permute-start(bf16[3,136,128]{2,1,0:T(8,128)(2,1)S(1)} %get-tuple-element.65), channel_id=1, source_target_pairs={{0,2},{2,0},{4,6},{6,4},{8,10},{10,8},{12,14},{14,12},{1,3},{3,1},... | collective-permute-start | bytes 313352 | tf_op jit(solution)/shard_map/cond/branch_1_fun/ppermute | solution.py:27
  26.3 12.2 %collective-permute-start.9 = (bf16[3,136,128]{2,1,0:T(8,128)(2,1)S(1)}, bf16[3,136,128]{2,1,0:T(8,128)(2,1)S(1)}, u32[]{:S(2)}, u32[]{:S(2)}) collective-permute-start(bf16[3,136,128]{2,1,0:T(8,128)(2,1)S(1)} %get-tuple-element.65), channel_id=1, source_target_pairs={{2,4},{4,2},{6,8},{8,6},{10,12},{12,10},{3,5},{5,3},{7,9},{9,7},{1... | collective-permute-start | bytes 313352 | tf_op jit(solution)/shard_map/cond/branch_1_fun/ppermute | solution.py:27

commit v4 on v3

--- a/solution.py
+++ b/solution.py
@@ -13,6 +13,7 @@
 SLOT = 24
 PER_TILE = 5
 PER_SENT = 3
+PER_SWEEP = 9
 SMALL_RUNG = 1
 ROW_BLOCK = 32
 F32 = jnp.float32
@@ -289,7 +290,7 @@
     return flags
 
 
-def smooth_kernel(count, info, coefs, field, fixed, halo, out, left, right, work, sides, near):
+def smooth_kernel(count, info, coefs, field, fixed, halo, out, left, right, work, near):
     levels, rows = left.shape[0], field.shape[1]
     deals = left.shape[1] // SUB
     flags = row_flags(info, deals, rows)
@@ -326,13 +327,15 @@
                 work[0, p, part, :LANES] = left[p, pl.ds(i, SUB, stride=deals), :]
                 work[0, p, part, LANES:] = right[p, pl.ds(i, SUB, stride=deals), :]
         for s in range(SMOOTH):
-            flat = work[s % 2].reshape(levels * deals * SUB, 2 * LANES).astype(BF16)
-            side = jnp.dot(flat, near[...], preferred_element_type=F32)
-            sides[...] = side.reshape(sides.shape)
             for p in range(levels):
+                first = p - p % PER_SENT
+                if p == first:
+                    flat = work[s % 2, p : p + PER_SENT].reshape(-1, 2 * LANES).astype(BF16)
+                    side = jnp.dot(flat, near[...], preferred_element_type=F32)
+                    side = side.reshape(PER_SENT, deals * SUB, 2 * LANES)
                 values = [work[s % 2, p, SUB * i : SUB * i + SUB, :] for i in range(deals)]
                 values = row_sweep(
-                    values, lambda i, _: sides[p, SUB * i : SUB * i + SUB, :], *weights[p]
+                    values, lambda i, _: side[p - first, SUB * i : SUB * i + SUB, :], *weights[p]
                 )
                 for i, value in enumerate(values):
                     if s == SMOOTH - 1:
@@ -547,10 +550,9 @@
         ],
         whole(parents, rows, columns),
         jax.ShapeDtypeStruct((parents, rows, columns), BF16),
-        [pltpu.VMEM((group, extended, LANES), F32)] * 2
+        [pltpu.VMEM((PER_SWEEP, extended, LANES), F32)] * 2
         + [
-            pltpu.VMEM((2, group, extended, columns), F32),
-            pltpu.VMEM((group, extended, columns), F32),
+            pltpu.VMEM((2, PER_SWEEP, extended, columns), F32),
             pltpu.VMEM((columns, columns), BF16),
         ],
         flops=1 << 34,

time: 43.4 us -> 42.8 us (0.986)
  Pallas kernels: 25.3 us -> 24.6 us
    pallas_call x1, Pallas kernels: 9.16 us -> 8.53 us  [feed_back(): call(functools.partial(smooth_kernel, count), (1,), [smem(), smem(), whol...]
  transfers between devices with their start and end apart: 5 -> 5, of which waited for: 1 -> 1; matrix products, arithmetic and copies ran while one was open for 1% -> 1% of each run, Pallas kernels for 32% -> 31%
where the time goes in v4:
time: 42.8 us; the launch traced here: 42.6 us
  Pallas kernels  24.6 us (57%)
  starting transfers between devices  12.2 us (29%)
  waiting for transfers between devices  3.12 us (7%)
  other arithmetic  1.45 us (3%)
  between operations  0.65 us (2%)
    ppermute x5, starting transfers between devices, pair_swap(): return lax.ppermute(x, axis, route)  12.2 us
    pallas_call x1, Pallas kernels, feed_back(): call(functools.partial(smooth_kernel, count), (1,), [smem(), smem(), whol...  8.53 us
    pallas_call x1, Pallas kernels, feed_back(): call(functools.partial(remap_kernel, count, total), (1,), [smem(), smem()...  5.32 us
    pallas_call x1, Pallas kernels, finish(): call(seam_kernel, (1,), [smem(), whole(2, seams, SUB, LANES), whole(sents...  4.69 us
    ppermute x5, waiting for transfers between devices, pair_swap(): return lax.ppermute(x, axis, route)  3.12 us
    pallas_call x1, Pallas kernels, feed_back(): call(functools.partial(edge_kernel, count), (rows // block,), [smem(), pl...  2.67 us
    pallas_call x1, Pallas kernels, feed_back(): call(functools.partial(blend_kernel, group), (1,), [whole(parents, rows,...  1.94 us
    reduce_max x1, other arithmetic, shards(): jnp.max(ends * jnp.array([1, -1]) + jnp.array([2 - parents, parents]))  1.42 us
  transfers between devices with their start and end apart: 5, of which 1 were waited for; matrix products, arithmetic and copies ran while one was open for 1% of the time, Pallas kernels for 31%

profile of v4, /device:TPU:35, one launch (start us, length us, event | category | flops | bytes accessed | tf_op | source)
XLA Modules:
  0.0 42.6 jit_solution(14834320337198978309)
XLA Ops:
  0.0 1.4 %add_reduce_fusion = s32[]{:T(128)} fusion(s32[2]{0:T(128)} %constant.124.clone, s32[2]{0:T(128)} %constant.123.clone, s32[136]{0:T(256)} %param.13), kind=kLoop, calls=%fused_computation.10 | loop fusion | flops 5 | bytes 28 | tf_op jit(solution)/shard_map/reduce_max | solution.py:607
  2.1 40.5 %conditional.1 = (bf16[45,128,256]{2,1,0:T(8,128)(2,1)}) conditional(s32[]{:T(128)} %convert_element_type.4, (f32[45]{0:T(128)}, s32[136]{0:T(256)}, f32[136]{0:T(256)}, f32[136]{0:T(256)}, bf16[68,128,256]{2,1,0:T(8,128)(2,1)}, /*index=5*/bf16[45,128,256]{2,1,0:T(8,128)(2,1)}, s32[128,256]{1,0:T(8,128)}) %tuple.11, (f32[45]{0:T(128)}, s32[136]{0:T(256)}, ...), branch_computations={%region_1.2_spmd, %region_2.3_spmd} | conditional | flops 51539615744 | bytes 39468136 | solution.py:614
  2.1 0.0 copy-start.5
  2.1 0.0 copy-start.3
  2.1 0.1 stack.92.info
  2.2 5.3 %branch_1_fun.7 = (bf16[45,128,256]{2,1,0:T(8,128)(2,1)S(1)}, bf16[1,128,256]{2,1,0:T(8,128)(2,1)S(1)}) custom-call(s32[8]{0:T(128)S(1)} %stack.92.info, s32[136]{0:T(256)} %get-tuple-element.54.begins.levels, s32[136]{0:T(256)} %get-tuple-element.54.begins.levels, f32[136]{0:T(256)} %get-tuple-element.55.inside, f32[136]{0:T(256)} %get-tuple-element.56.thick, ...), custom_call_target="tpu_custom_call" | custom-call | flops 1 | bytes 1048576 | tf_op jit(solution)/shard_map/cond/branch_1_fun/pallas_call | solution.py:440
  7.6 1.4 %collective-permute-start.5 = (bf16[1,128,256]{2,1,0:T(8,128)(2,1)S(1)}, bf16[1,128,256]{2,1,0:T(8,128)(2,1)S(1)}, u32[]{:S(2)}, u32[]{:S(2)}) collective-permute-start(bf16[1,128,256]{2,1,0:T(8,128)(2,1)S(1)} %get-tuple-element.61), channel_id=1, source_target_pairs={{0,1},{1,0},{2,3},{3,2},{4,5},{5,4},{6,7},{7,6},{8,9},{9,8},{10,11... | collective-permute-start | bytes 196616 | tf_op jit(solution)/shard_map/cond/branch_1_fun/ppermute | solution.py:28
  9.0 0.0 copy-done.5
  9.0 0.1 reshape.44
  9.0 0.1 broadcast_in_dim.29
  9.1 0.1 reshape.45
  9.2 0.0 copy-done.3
  9.2 1.9 %branch_1_fun.8.field_t.field_b.field = bf16[45,128,256]{2,1,0:T(8,128)(2,1)S(1)} custom-call(bf16[45,128,256]{2,1,0:T(8,128)(2,1)S(1)} %get-tuple-element.58.own, bf16[45,128,256]{2,1,0:T(8,128)(2,1)} %get-tuple-element.59.par, s32[128,256]{1,0:T(8,128)S(1)} %copy-done.3), custom_call_target="tpu_custom_call" | custom-call | flops 17179869184 | bytes 1048576 | tf_op jit(solution)/shard_map/cond/branch_1_fun/pallas_call | solution.py:462
  11.2 0.0 collective-permute-done.5.part_t.part_b.part
  11.2 0.7 %branch_1_fun.9 = (bf16[23,8,256]{2,1,0:T(8,128)(2,1)S(1)}, bf16[23,8,256]{2,1,0:T(8,128)(2,1)S(1)}) custom-call(s32[8]{0:T(128)S(1)} %stack.92.info, bf16[45,128,256]{2,1,0:T(8,128)(2,1)S(1)} %branch_1_fun.8.field_t.field_b.field, bf16[45,128,256]{2,1,0:T(8,128)(2,1)S(1)} %branch_1_fun.8.field_t.field_b.field, s32[128,256]{1,0:T(8,128)S(1)} %copy-done.3, ...), custom_call_target="tpu_custom_call" | custom-call | flops 1 | bytes 1048576 | tf_op jit(solution)/shard_map/cond/branch_1_fun/pallas_call | solution.py:485
  11.9 2.7 %collective-permute-start.6 = (bf16[23,8,256]{2,1,0:T(8,128)(2,1)S(1)}, bf16[23,8,256]{2,1,0:T(8,128)(2,1)S(1)}, u32[]{:S(2)}, u32[]{:S(2)}) collective-permute-start(bf16[23,8,256]{2,1,0:T(8,128)(2,1)S(1)} %get-tuple-element.62), channel_id=1, source_target_pairs={{0,16},{16,0},{32,48},{48,32},{64,80},{80,64},{96,112},{112,96},{1... | collective-permute-start | bytes 282632 | tf_op jit(solution)/shard_map/cond/branch_1_fun/ppermute | solution.py:28
  14.6 1.9 %collective-permute-start.7 = (bf16[23,8,256]{2,1,0:T(8,128)(2,1)S(1)}, bf16[23,8,256]{2,1,0:T(8,128)(2,1)S(1)}, u32[]{:S(2)}, u32[]{:S(2)}) collective-permute-start(bf16[23,8,256]{2,1,0:T(8,128)(2,1)S(1)} %get-tuple-element.63), channel_id=1, source_target_pairs={{16,32},{32,16},{48,64},{64,48},{80,96},{96,80},{17,33},{33,17},{4... | collective-permute-start | bytes 282632 | tf_op jit(solution)/shard_map/cond/branch_1_fun/ppermute | solution.py:28
  16.5 2.7 %branch_1_fun.10 = (bf16[1,128,256]{2,1,0:T(8,128)(2,1)S(1)}, bf16[9,128,128]{2,1,0:T(8,128)(2,1)S(1)}, bf16[3,128,128]{2,1,0:T(8,128)(2,1)S(1)}) custom-call(s32[8]{0:T(128)S(1)} %stack.92.info, bf16[45,128,256]{2,1,0:T(8,128)(2,1)S(1)} %branch_1_fun.8.field_t.field_b.field, s32[128,256]{1,0:T(8,128)S(1)} %copy-done.3, ...), custom_call_target="tpu_custom_call" | custom-call | flops 17179869184 | bytes 1048576 | tf_op jit(solution)/shard_map/cond/branch_1_fun/pallas_call | solution.py:504
  19.2 0.0 collective-permute-done.6.even
  19.2 3.1 %collective-permute-done.7.odd = bf16[23,8,256]{2,1,0:T(8,128)(2,1)S(1)} collective-permute-done((bf16[23,8,256]{2,1,0:T(8,128)(2,1)S(1)}, bf16[23,8,256]{2,1,0:T(8,128)(2,1)S(1)}, u32[]{:S(2)}, u32[]{:S(2)}) %collective-permute-start.7) | collective-permute-done | bytes 94240 | tf_op jit(solution)/shard_map/cond/branch_1_fun/ppermute | solution.py:28
  22.3 0.8 %branch_1_fun.11 = (bf16[45,8,256]{2,1,0:T(8,128)(2,1)S(1)}, bf16[9,8,128]{2,1,0:T(8,128)(2,1)S(1)}, bf16[3,136,128]{2,1,0:T(8,128)(2,1)S(1)}) custom-call(s32[8]{0:T(128)S(1)} %stack.92.info, bf16[23,8,256]{2,1,0:T(8,128)(2,1)S(1)} %collective-permute-done.6.even, bf16[23,8,256]{2,1,0:T(8,128)(2,1)S(1)} %collective-permute-done.7.odd, ...), custom_call_target="tpu_custom_call" | custom-call | flops 1 | bytes 1048576 | tf_op jit(solution)/shard_map/cond/branch_1_fun/pallas_call | solution.py:527
  23.1 3.2 %collective-permute-start.8 = (bf16[3,136,128]{2,1,0:T(8,128)(2,1)S(1)}, bf16[3,136,128]{2,1,0:T(8,128)(2,1)S(1)}, u32[]{:S(2)}, u32[]{:S(2)}) collective-permute-start(bf16[3,136,128]{2,1,0:T(8,128)(2,1)S(1)} %get-tuple-element.65), channel_id=1, source_target_pairs={{0,2},{2,0},{4,6},{6,4},{8,10},{10,8},{12,14},{14,12},{1,3},{3,1},... | collective-permute-start | bytes 313352 | tf_op jit(solution)/shard_map/cond/branch_1_fun/ppermute | solution.py:28
  26.3 3.0 %collective-permute-start.9 = (bf16[3,136,128]{2,1,0:T(8,128)(2,1)S(1)}, bf16[3,136,128]{2,1,0:T(8,128)(2,1)S(1)}, u32[]{:S(2)}, u32[]{:S(2)}) collective-permute-start(bf16[3,136,128]{2,1,0:T(8,128)(2,1)S(1)} %get-tuple-element.65), channel_id=1, source_target_pairs={{2,4},{4,2},{6,8},{8,6},{10,12},{12,10},{3,5},{5,3},{7,9},{9,7},{1... | collective-permute-start | bytes 313352 | tf_op jit(solution)/shard_map/cond/branch_1_fun/ppermute | solution.py:28
  29.3 8.5 %branch_1_fun.12.main = bf16[45,128,256]{2,1,0:T(8,128)(2,1)S(1)} custom-call(s32[8]{0:T(128)S(1)} %stack.92.info, f32[45]{0:T(128)S(1)} %copy-done.5, bf16[45,128,256]{2,1,0:T(8,128)(2,1)S(1)} %branch_1_fun.8.field_t.field_b.field, bf16[1,128,256]{2,1,0:T(8,128)(2,1)S(1)} %get-tuple-element.68.fixed, bf16[45,8,256]{2,1,0:T(8,128)(2,1)S(1)} %get-tuple-element.69.halo), custom_call_target="tpu_custom_call" | custom-call | flops 17179869184 | bytes 1048576 | tf_op jit(solution)/shard_map/cond/branch_1_fun/pallas_call | solution.py:542
  37.8 0.0 collective-permute-done.8.even
  37.9 0.0 collective-permute-done.9.odd
  37.9 4.7 %branch_1_fun.13 = bf16[45,128,256]{2,1,0:T(8,128)(2,1)} custom-call(s32[8]{0:T(128)S(1)} %stack.92.info, f32[2,9,8,128]{3,2,1,0:T(8,128)S(1)} %broadcast_in_dim.31.coefs, bf16[3,136,128]{2,1,0:T(8,128)(2,1)S(1)} %collective-permute-done.8.even, bf16[3,136,128]{2,1,0:T(8,128)(2,1)S(1)} %collective-permute-done.9.odd, ...), custom_call_target="tpu_custom_call" | custom-call | flops 1 | bytes 1048576 | tf_op jit(solution)/shard_map/cond/branch_1_fun/pallas_call | solution.py:580
  (4 shorter events, 0.0 us)
Async XLA Ops:
  2.1 6.9 %copy-start.5 = (f32[45]{0:T(128)S(1)}, f32[45]{0:T(128)}, u32[]{:S(2)}) copy-start(f32[45]{0:T(128)} %get-tuple-element.53.coefs) | copy-start | bytes 544 | tf_op jit(solution)/shard_map/cond
  2.1 7.1 %copy-start.3 = (s32[128,256]{1,0:T(8,128)S(1)}, s32[128,256]{1,0:T(8,128)}, u32[]{:S(2)}) copy-start(s32[128,256]{1,0:T(8,128)} %get-tuple-element.60.mask.mask_t.mask_b) | copy-start | bytes 393220 | tf_op jit(solution)/shard_map/cond
  7.6 3.6 %collective-permute-start.5 = (bf16[1,128,256]{2,1,0:T(8,128)(2,1)S(1)}, bf16[1,128,256]{2,1,0:T(8,128)(2,1)S(1)}, u32[]{:S(2)}, u32[]{:S(2)}) collective-permute-start(bf16[1,128,256]{2,1,0:T(8,128)(2,1)S(1)} %get-tuple-element.61), channel_id=1, source_target_pairs={{0,1},{1,0},{2,3},{3,2},{4,5},{5,4},{6,7},{7,6},{8,9},{9,8},{10,11... | collective-permute-start | bytes 196616 | tf_op jit(solution)/shard_map/cond/branch_1_fun/ppermute | solution.py:28
  11.9 7.3 %collective-permute-start.6 = (bf16[23,8,256]{2,1,0:T(8,128)(2,1)S(1)}, bf16[23,8,256]{2,1,0:T(8,128)(2,1)S(1)}, u32[]{:S(2)}, u32[]{:S(2)}) collective-permute-start(bf16[23,8,256]{2,1,0:T(8,128)(2,1)S(1)} %get-tuple-element.62), channel_id=1, source_target_pairs={{0,16},{16,0},{32,48},{48,32},{64,80},{80,64},{96,112},{112,96},{1... | collective-permute-start | bytes 282632 | tf_op jit(solution)/shard_map/cond/branch_1_fun/ppermute | solution.py:28
  14.6 7.7 %collective-permute-start.7 = (bf16[23,8,256]{2,1,0:T(8,128)(2,1)S(1)}, bf16[23,8,256]{2,1,0:T(8,128)(2,1)S(1)}, u32[]{:S(2)}, u32[]{:S(2)}) collective-permute-start(bf16[23,8,256]{2,1,0:T(8,128)(2,1)S(1)} %get-tuple-element.63), channel_id=1, source_target_pairs={{16,32},{32,16},{48,64},{64,48},{80,96},{96,80},{17,33},{33,17},{4... | collective-permute-start | bytes 282632 | tf_op jit(solution)/shard_map/cond/branch_1_fun/ppermute | solution.py:28
  23.1 14.8 %collective-permute-start.8 = (bf16[3,136,128]{2,1,0:T(8,128)(2,1)S(1)}, bf16[3,136,128]{2,1,0:T(8,128)(2,1)S(1)}, u32[]{:S(2)}, u32[]{:S(2)}) collective-permute-start(bf16[3,136,128]{2,1,0:T(8,128)(2,1)S(1)} %get-tuple-element.65), channel_id=1, source_target_pairs={{0,2},{2,0},{4,6},{6,4},{8,10},{10,8},{12,14},{14,12},{1,3},{3,1},... | collective-permute-start | bytes 313352 | tf_op jit(solution)/shard_map/cond/branch_1_fun/ppermute | solution.py:28
  26.3 11.6 %collective-permute-start.9 = (bf16[3,136,128]{2,1,0:T(8,128)(2,1)S(1)}, bf16[3,136,128]{2,1,0:T(8,128)(2,1)S(1)}, u32[]{:S(2)}, u32[]{:S(2)}) collective-permute-start(bf16[3,136,128]{2,1,0:T(8,128)(2,1)S(1)} %get-tuple-element.65), channel_id=1, source_target_pairs={{2,4},{4,2},{6,8},{8,6},{10,12},{12,10},{3,5},{5,3},{7,9},{9,7},{1... | collective-permute-start | bytes 313352 | tf_op jit(solution)/shard_map/cond/branch_1_fun/ppermute | solution.py:28
